TPU v7x, 128 devices: a whole 4x4x4 slice. The times are simulated.
128 devices in a mesh: dp: 16 (over x, z), tensor: 8 (over y, core).
Axes of the slice: x: 4, y: 4, z: 4, core: 2. Of those that a mesh axis runs over, the one named last changes fastest.
Arguments:
- tokens: bfloat16 [1024, 4096], P('dp', 'tensor')
- norm_gain: float32 [4096], P('tensor'), may hold values from 0.5 to 1.5
- eraser_mean: float32 [4096], P('tensor'), may hold values from -6 to 6
- eraser_in: float32 [4096, 128], P('tensor'), may hold values from -0.09375 to 0.09375
- eraser_out: float32 [4096, 128], P('tensor'), may hold values from -0.5 to 0.5
- router: float32 [4096, 8], P('tensor'), may hold values from -0.09375 to 0.09375
- expert_ids: int32 [1024, 2], P('dp'), may hold values from 0 to 7, as said below
- slots: int32 [1024, 2], P('dp'), may hold values from 0 to 63, as said below
- w_gate: bfloat16 [16, 4096, 7168], P('dp', None, 'tensor'), may hold values from -0.09375 to 0.09375
- w_up: bfloat16 [16, 4096, 7168], P('dp', None, 'tensor'), may hold values from -0.09375 to 0.09375
- w_down: bfloat16 [16, 7168, 4096], P('dp', 'tensor'), may hold values from -0.0625 to 0.0625
Outputs:
- moe_out: bfloat16 [1024, 4096], P('dp', 'tensor')
Inputs may be any that keep to these rules, and one draw needn't show every extreme that they name: `expert_ids`: the two experts of a token differ. Within each aligned block of 64 tokens, the choices naming one expert have the slots 0, 1, 2, ... with no repeats; choices with a slot of 24 or more are dropped.
All inputs are finite; a program needn't handle non-finite values.
Results may differ from a plain program's by a relative error of at most 0.0065.
Values may be sent and summed in bfloat16 or wider, within the bound.
No kernel may reach another device: no remote copies, remote signals or barrier semaphores. Data moves between devices by JAX's collectives and lax.ppermute only.
A program may use at most 128 MiB of HBM per device.

v0:
```python
import jax
import jax.numpy as jnp
from jax import lax
from jax.experimental import pallas as pl
from jax.sharding import PartitionSpec as P

E = 8
HIGHEST = lax.Precision.HIGHEST


def dot32(a, b):
    return jnp.dot(a, b, precision=HIGHEST, preferred_element_type=jnp.float32)


def dot32_nt(a, b):
    return lax.dot_general(a, b, (((1,), (1,)), ((), ())), precision=HIGHEST, preferred_element_type=jnp.float32)


def sums_kernel(tokens, gain, mean, eraser_in, eraser_out, router_t, out):
    rows = tokens.shape[0]
    values = tokens[...].astype(jnp.float32)
    gained = values * gain[...]
    out[:rows] = dot32(gained, eraser_in[...])
    out[rows : rows + 8] = dot32(jnp.broadcast_to(mean[...], (8, mean.shape[1])), eraser_in[...])
    out[rows + 8 : rows + 16] = dot32(router_t[...], eraser_out[...])
    out[rows + 16 : rows + 24, :rows] = dot32_nt(router_t[...], gained)
    out[rows + 16 : rows + 24, rows : 2 * rows] = dot32_nt(jnp.ones((8, values.shape[1]), jnp.float32), values * values)


def on_device(tokens, norm_gain, eraser_mean, eraser_in, eraser_out, router, expert_ids, slots, w_gate, w_up, w_down):
    bf = jnp.bfloat16
    f32 = jnp.float32
    n_t = lax.axis_size("tensor")
    n_y = n_t // 2
    part_count = lax.axis_size("dp") // E
    rows, width = tokens.shape
    capacity = 3 * rows // 8
    full = width * n_t
    total = lax.axis_size("dp") * capacity
    rank = eraser_in.shape[1]
    t = lax.axis_index("tensor")
    y, c = t // 2, t % 2

    def along_y(v, k):
        return lax.ppermute(v, "tensor", [(s, ((s // 2 + k) % n_y) * 2 + s % 2) for s in range(n_t)])

    def to_twin(v):
        return lax.ppermute(v, "tensor", [(s, s ^ 1) for s in range(n_t)])

    target = jnp.where(slots < capacity, expert_ids * capacity + slots, -1)
    place = jnp.arange(total, dtype=jnp.int32)
    place = (place // capacity // part_count) * capacity + place % capacity
    match = target.T[:, None, :] == place[None, :, None]
    placing = lax.optimization_barrier(jnp.any(match, axis=0).astype(bf))
    packed = pl.pallas_call(
        sums_kernel, out_shape=jax.ShapeDtypeStruct((rows + 24, rank), f32), name="sums"
    )(tokens, norm_gain[None, :], eraser_mean[None, :], eraser_in, eraser_out, router.T)
    packed = packed + to_twin(packed)
    sums = (packed + along_y(packed, 2)) + (along_y(packed, 1) + along_y(packed, -1))
    mean_in = sums[rows : rows + 1]
    out_router_t = sums[rows + 8 : rows + 16]
    inv_rms = lax.rsqrt(sums[rows + 16, rows : 2 * rows] / full + 1e-05)
    projected = inv_rms[:, None] * sums[:rows] - mean_in
    gained = tokens.astype(f32) * norm_gain[None, :]
    erased = (inv_rms[:, None] * gained - dot32_nt(projected, eraser_out)).astype(bf)
    sent = jnp.dot(placing, erased, preferred_element_type=f32).astype(bf)
    own = lax.all_to_all(sent.reshape(-1, capacity, width), "dp", split_axis=0, concat_axis=0, tiled=True)
    own = own.reshape(total, width)

    logits = inv_rms[:, None] * sums[rows + 16 : rows + 24, :rows].T - lax.dot_general(
        projected, out_router_t, (((1,), (1,)), ((), ())), precision=HIGHEST, preferred_element_type=f32
    )
    chosen = (expert_ids[:, :, None] == jnp.arange(E, dtype=jnp.int32)[None, None, :]).astype(f32)
    picked = jnp.sum(chosen * logits[:, None, :], axis=2)
    first_gate = jax.nn.sigmoid(picked[:, 0] - picked[:, 1])
    gate_pair = jnp.stack([first_gate, 1.0 - first_gate], axis=1)
    weights = jnp.sum((target[:, :, None] == place[None, None, :]).astype(f32) * gate_pair[:, :, None], axis=1)

    half = total // 2
    wg, wu, wd = w_gate[0], w_up[0], w_down[0]

    def rows_of(w, k, core):
        return lax.dynamic_slice_in_dim(w, (((y + k) % n_y) * 2 + core) * width, width, 0)

    def cols_of(w, k, core):
        return lax.dynamic_slice_in_dim(w, (((y + k) % n_y) * 2 + core) * width, width, 1)

    def dot(p, q):
        return jnp.dot(p, q, preferred_element_type=f32)

    def add_to(acc, *pieces):
        for piece, k, core in pieces:
            g = dot(piece, rows_of(wg, k, core))
            u = dot(piece, rows_of(wu, k, core))
            acc = (g, u) if acc is None else (acc[0] + g, acc[1] + u)
        return acc

    up_a = along_y(own[:half], 1)
    down_b = along_y(own[half:], -1)
    up_b = along_y(own[half:], 1)
    down_a = along_y(own[:half], -1)
    own2 = to_twin(own)
    acc = add_to(None, (own, 0, c), (own2, 0, 1 - c))
    far_a = along_y(up_a, 1)
    far_b = along_y(down_b, -1)
    up = jnp.concatenate([up_a, up_b], axis=0)
    down = jnp.concatenate([down_a, down_b], axis=0)
    up, down, acc = lax.optimization_barrier((up, down, acc))
    up2 = to_twin(up)
    down2 = to_twin(down)
    acc = add_to(acc, (up, -1, c), (down, 1, c), (up2, -1, 1 - c), (down2, 1, 1 - c))
    far_a, far_b, acc = lax.optimization_barrier((far_a, far_b, acc))
    far = jnp.concatenate([far_a, far_b], axis=0)
    far2 = to_twin(far)
    gate_act, up_act = add_to(acc, (far, 2, c), (far2, 2, 1 - c))
    hidden = (jax.nn.silu(gate_act) * up_act).astype(bf)

    def summed(k):
        other = dot(hidden, cols_of(wd, k, 1 - c)).astype(bf)
        return dot(hidden, cols_of(wd, k, c)) + to_twin(other).astype(f32)

    far = summed(2).astype(bf)
    got_far_a = along_y(far[:half], 1)
    got_far_b = along_y(far[half:], -1)
    to_up = summed(1)
    to_down = summed(-1)
    got_b = along_y(to_up[half:].astype(bf), 1)
    got_a = along_y(to_down[:half].astype(bf), -1)
    mine = summed(0)
    last_a = along_y((to_up[:half] + got_far_a.astype(f32)).astype(bf), 1)
    last_b = along_y((to_down[half:] + got_far_b.astype(f32)).astype(bf), -1)
    reduced = mine + jnp.concatenate(
        [last_a.astype(f32) + got_a.astype(f32), got_b.astype(f32) + last_b.astype(f32)], axis=0
    )
    returned = lax.all_to_all(
        reduced.astype(bf).reshape(-1, capacity, width), "dp", split_axis=0, concat_axis=0, tiled=True
    )
    mixed = jnp.dot(weights, returned.reshape(total, width).astype(f32), precision=HIGHEST, preferred_element_type=f32)
    return mixed.astype(bf)


def solution(mesh):
    in_specs = (
        P("dp", "tensor"),
        P("tensor"),
        P("tensor"),
        P("tensor", None),
        P("tensor", None),
        P("tensor", None),
        P("dp", None),
        P("dp", None),
        P("dp", None, "tensor"),
        P("dp", None, "tensor"),
        P("dp", "tensor", None),
    )

    return jax.shard_map(on_device, mesh=mesh, in_specs=in_specs, out_specs=P("dp", "tensor"), check_vma=False)
```

profile of v0, /device:TPU:0, one launch (start us, length us, event | category | flops | bytes accessed | tf_op | source)
XLA Modules:
  0.0 100.6 jit_solution(12163870690425495100)
XLA Ops:
  0.0 2.5 %sums.1 = f32[88,128]{1,0:T(8,128)} custom-call(bf16[64,512]{1,0:T(8,128)(2,1)} %tokens.1, f32[1,512]{1,0:T(1,128)} %bitcast.148, f32[1,512]{1,0:T(1,128)} %bitcast.149, f32[512,128]{1,0:T(8,128)} %eraser_in.1, f32[512,128]{1,0:T(8,128)} %eraser_out.1, f32[8,512]{1,0:T(8,128)} %bitcast.146), custom_call_target="tpu_custom_call" | custom-call | tf_op jit(solution)/shard_map/sums/pallas_call | solution.py:55
  2.5 0.8 compare_select_fusion
  3.3 0.7 collective-permute-done
  3.9 0.8 add.295
  4.7 3.3 %collective-permute-start.1 = (f32[88,128]{1,0:T(8,128)S(1)}, f32[88,128]{1,0:T(8,128)S(1)}, u32[]{:S(2)}, u32[]{:S(2)}) collective-permute-start(f32[88,128]{1,0:T(8,128)S(1)} %add.295), channel_id=1, source_target_pairs={{0,4},{1,5},{2,6},{3,7},{4,0},{5,1},{6,2},{7,3},{8,12},{9,13},{10,... | collective-permute-start | bytes 135176 | tf_op jit(solution)/shard_map/ppermute | solution.py:45
  8.0 0.7 collective-permute-start.2
  8.7 2.6 %collective-permute-start.3 = (f32[88,128]{1,0:T(8,128)S(1)}, f32[88,128]{1,0:T(8,128)S(1)}, u32[]{:S(2)}, u32[]{:S(2)}) collective-permute-start(f32[88,128]{1,0:T(8,128)S(1)} %add.295), channel_id=1, source_target_pairs={{0,6},{1,7},{2,0},{3,1},{4,2},{5,3},{6,4},{7,5},{8,14},{9,15},{10,... | collective-permute-start | bytes 135176 | tf_op jit(solution)/shard_map/ppermute | solution.py:45
  11.4 1.9 %collective-permute-done.2 = f32[88,128]{1,0:T(8,128)S(1)} collective-permute-done((f32[88,128]{1,0:T(8,128)S(1)}, f32[88,128]{1,0:T(8,128)S(1)}, u32[]{:S(2)}, u32[]{:S(2)}) %collective-permute-start.2) | collective-permute-done | bytes 45088 | tf_op jit(solution)/shard_map/ppermute | solution.py:45
  13.4 1.4 %fusion.2 = bf16[64,512]{1,0:T(8,128)(2,1)S(1)} fusion(f32[512,128]{1,0:T(8,128)} %eraser_out.1, bf16[64,512]{1,0:T(8,128)(2,1)} %tokens.1, f32[512]{0:T(512)} %param.12, f32[64]{0:T(128)S(1)} %fusion.136, f32[88,128]{1,0:T(8,128)S(1)} %add_add_fusion, f32[128]{0:T(128)S(1)} %slice_bitcast_fusion), kind=kOutput, calls=%fused_computation.15 | convolution fusion | flops 50511872 | bytes 429568 | tf_op jit(solution)/shard_map/dot_general | solution.py:16
  14.8 1.0 %convolution_convert_fusion.4 = bf16[384,512]{1,0:T(8,128)(2,1)} fusion(bf16[384,64]{0,1:T(8,128)(2,1)S(1)} %convert_element_type.77, bf16[64,512]{1,0:T(8,128)(2,1)S(1)} %fusion.2), kind=kOutput, calls=%fused_computation.13 | convolution fusion | flops 25362432 | bytes 507904 | tf_op jit(solution)/shard_map/dot_general | solution.py:66
  15.9 8.0 %all-to-all-start = ((bf16[16,24,512]{2,1,0:T(8,128)(2,1)}), bf16[16,24,512]{2,1,0:T(8,128)(2,1)S(1)}, u32[]{:S(2)}, u32[]{:S(2)}) async-start(bf16[16,24,512]{2,1,0:T(8,128)(2,1)} %bitcast.139), calls=%async_computation | async-start | bytes 786432 | tf_op jit(solution)/shard_map/all_to_all | solution.py:67
  24.0 1.0 fusion.122
  25.0 8.0 %all-to-all-done = bf16[16,24,512]{2,1,0:T(8,128)(2,1)S(1)} async-done(((bf16[16,24,512]{2,1,0:T(8,128)(2,1)}), bf16[16,24,512]{2,1,0:T(8,128)(2,1)S(1)}, u32[]{:S(2)}, u32[]{:S(2)}) %all-to-all-start) | async-done | bytes 393248 | tf_op jit(solution)/shard_map/all_to_all | solution.py:67
  33.0 3.3 %collective-permute-start.9 = (bf16[192,512]{1,0:T(8,128)(2,1)S(1)}, bf16[192,512]{1,0:T(8,128)(2,1)S(1)}, u32[]{:S(2)}, u32[]{:S(2)}) collective-permute-start(bf16[192,512]{1,0:T(8,128)(2,1)S(1)} %bitcast.144), channel_id=1, source_target_pairs={{0,6},{1,7},{2,0},{3,1},{4,2},{5,3},{6,4},{7,5},{8,14},{9,15},{10,... | collective-permute-start | bytes 589832 | tf_op jit(solution)/shard_map/ppermute | solution.py:45
  36.3 3.2 %collective-permute-start.6 = (bf16[192,512]{1,0:T(8,128)(2,1)S(1)}, bf16[192,512]{1,0:T(8,128)(2,1)S(1)}, u32[]{:S(2)}, u32[]{:S(2)}) collective-permute-start(bf16[192,512]{1,0:T(8,128)(2,1)S(1)} %bitcast.142), channel_id=1, source_target_pairs={{0,6},{1,7},{2,0},{3,1},{4,2},{5,3},{6,4},{7,5},{8,14},{9,15},{10,... | collective-permute-start | bytes 589832 | tf_op jit(solution)/shard_map/ppermute | solution.py:45
  39.6 1.7 %fusion.57 = f32[384,896]{1,0:T(8,128)S(1)} fusion(bf16[384,512]{1,0:T(8,128)(2,1)S(1)} %bitcast.136, bf16[1,4096,896]{2,1,0:T(8,128)(2,1)} %param.20, s32[]{:T(128)S(6)} %select_n.162), kind=kOutput, calls=%fused_computation.57 | convolution fusion | flops 352321536 | bytes 2686980 | tf_op jit(solution)/shard_map/dot_general | solution.py:89
  41.3 1.9 %fusion.60 = f32[384,896]{1,0:T(8,128)S(1)} fusion(bf16[384,512]{1,0:T(8,128)(2,1)S(1)} %bitcast.137, bf16[1,4096,896]{2,1,0:T(8,128)(2,1)} %param.19, s32[]{:T(128)S(6)} %select_n.162), kind=kOutput, calls=%fused_computation.60 | convolution fusion | flops 352321536 | bytes 2686980 | tf_op jit(solution)/shard_map/dot_general | solution.py:89
  43.8 3.2 %collective-permute-start.7 = (bf16[192,512]{1,0:T(8,128)(2,1)S(1)}, bf16[192,512]{1,0:T(8,128)(2,1)S(1)}, u32[]{:S(2)}, u32[]{:S(2)}) collective-permute-start(bf16[192,512]{1,0:T(8,128)(2,1)S(1)} %collective-permute-done.6), channel_id=1, source_target_pairs={{0,6},{1,7},{2,0},{3,1},{4,2},{5,3},{6,4},{7,5},{8,14},{9,15},{10,... | collective-permute-start | bytes 589832 | tf_op jit(solution)/shard_map/ppermute | solution.py:45
  47.2 1.9 %convolution_add_fusion.4 = f32[384,896]{1,0:T(8,128)S(1)} fusion(f32[384,896]{1,0:T(8,128)S(1)} %fusion.57, bf16[384,512]{1,0:T(8,128)(2,1)S(1)} %collective-permute-done.10, bf16[1,4096,896]{2,1,0:T(8,128)(2,1)} %param.20, s32[]{:T(128)S(6)} %select_n.163), kind=kOutput, calls=%fused_computation.4 | convolution fusion | flops 352665600 | bytes 4063236 | tf_op jit(solution)/shard_map/dot_general | solution.py:89
  49.8 0.7 copy-done
  55.4 0.7 collective-permute-start.13
  59.7 1.2 %slice-done.3 = s8[3145728]{0:T(1024)(128)(4,1)S(1)} async-done(((s8[7340032]{0:T(1024)(128)(4,1)}), s8[3145728]{0:T(1024)(128)(4,1)S(1)}, s32[]{:S(2)}) %slice-start.3) | async-done | bytes 3145752
  65.8 3.3 %collective-permute-start.20 = (bf16[192,512]{1,0:T(8,128)(2,1)S(1)}, bf16[192,512]{1,0:T(8,128)(2,1)S(1)}, u32[]{:S(2)}, u32[]{:S(2)}) collective-permute-start(bf16[192,512]{1,0:T(8,128)(2,1)S(1)} %slice.116), channel_id=1, source_target_pairs={{0,6},{1,7},{2,0},{3,1},{4,2},{5,3},{6,4},{7,5},{8,14},{9,15},{10,... | collective-permute-start | bytes 589832 | tf_op jit(solution)/shard_map/ppermute | solution.py:45
  69.8 3.2 %collective-permute-start.22 = (bf16[192,512]{1,0:T(8,128)(2,1)S(1)}, bf16[192,512]{1,0:T(8,128)(2,1)S(1)}, u32[]{:S(2)}, u32[]{:S(2)}) collective-permute-start(bf16[192,512]{1,0:T(8,128)(2,1)S(1)} %get-tuple-element.24), channel_id=1, source_target_pairs={{0,6},{1,7},{2,0},{3,1},{4,2},{5,3},{6,4},{7,5},{8,14},{9,15},{10,... | collective-permute-start | bytes 589832 | tf_op jit(solution)/shard_map/ppermute | solution.py:45
  73.0 0.7 collective-permute-done.17
  73.9 3.9 %collective-permute-done.22 = bf16[192,512]{1,0:T(8,128)(2,1)S(1)} collective-permute-done((bf16[192,512]{1,0:T(8,128)(2,1)S(1)}, bf16[192,512]{1,0:T(8,128)(2,1)S(1)}, u32[]{:S(2)}, u32[]{:S(2)}) %collective-permute-start.22) | collective-permute-done | bytes 196640 | tf_op jit(solution)/shard_map/ppermute | solution.py:45
  77.8 3.8 %collective-permute-start.23 = (bf16[192,512]{1,0:T(8,128)(2,1)S(1)}, bf16[192,512]{1,0:T(8,128)(2,1)S(1)}, u32[]{:S(2)}, u32[]{:S(2)}) collective-permute-start(bf16[192,512]{1,0:T(8,128)(2,1)S(1)} %fusion.86), channel_id=1, source_target_pairs={{0,6},{1,7},{2,0},{3,1},{4,2},{5,3},{6,4},{7,5},{8,14},{9,15},{10,... | collective-permute-start | bytes 589832 | tf_op jit(solution)/shard_map/ppermute | solution.py:45
  82.1 3.1 %collective-permute-done.23 = bf16[192,512]{1,0:T(8,128)(2,1)S(1)} collective-permute-done((bf16[192,512]{1,0:T(8,128)(2,1)S(1)}, bf16[192,512]{1,0:T(8,128)(2,1)S(1)}, u32[]{:S(2)}, u32[]{:S(2)}) %collective-permute-start.23) | collective-permute-done | bytes 196640 | tf_op jit(solution)/shard_map/ppermute | solution.py:45
  85.2 1.3 %fusion.33 = bf16[384,512]{1,0:T(8,128)(2,1)} fusion(bf16[384,896]{1,0:T(8,128)(2,1)S(1)} %multiply_convert_fusion, bf16[1,896,4096]{2,1,0:T(8,128)(2,1)S(1)} %bitcast.141, s32[]{:T(128)S(6)} %select_n.162, f32[192,512]{1,0:T(8,128)S(1)} %convert_add_fusion, f32[192,512]{1,0:T(8,128)S(1)} %convert_add_fusion.1, bf16[384,512]{1,0:T(8,128)(2,1)S(1)} %collective-permute-done.14), kind=kOutput, calls=%fused_computation.35 | convolution fusion | flops 353304576 | bytes 3178500 | tf_op jit(solution)/shard_map/dot_general | solution.py:89
  86.6 4.0 %all-to-all-start.1 = ((bf16[16,24,512]{2,1,0:T(8,128)(2,1)}), bf16[16,24,512]{2,1,0:T(8,128)(2,1)S(1)}, u32[]{:S(2)}, u32[]{:S(2)}) async-start(bf16[16,24,512]{2,1,0:T(8,128)(2,1)} %bitcast.35), calls=%async_computation.1 | async-start | bytes 786432 | tf_op jit(solution)/shard_map/all_to_all | solution.py:135
  90.7 9.0 %all-to-all-done.1 = bf16[16,24,512]{2,1,0:T(8,128)(2,1)S(1)} async-done(((bf16[16,24,512]{2,1,0:T(8,128)(2,1)}), bf16[16,24,512]{2,1,0:T(8,128)(2,1)S(1)}, u32[]{:S(2)}, u32[]{:S(2)}) %all-to-all-start.1) | async-done | bytes 393248 | tf_op jit(solution)/shard_map/all_to_all | solution.py:135
  99.7 1.0 convolution_convert_fusion.5
  (92 shorter events, 16.3 us)
Async XLA Ops:
  2.5 22.5 %copy-start.2 = (s32[64,2]{0,1:T(2,128)S(1)}, s32[64,2]{0,1:T(2,128)}, u32[]{:S(2)}) copy-start(s32[64,2]{0,1:T(2,128)} %param.17) | copy-start | bytes 1540
  2.5 1.4 %collective-permute-start = (f32[88,128]{1,0:T(8,128)}, f32[88,128]{1,0:T(8,128)S(1)}, u32[]{:S(2)}, u32[]{:S(2)}) collective-permute-start(f32[88,128]{1,0:T(8,128)} %sums.1), channel_id=1, source_target_pairs={{0,1},{1,0},{2,3},{3,2},{4,5},{5,4},{6,7},{7,6},{8,9},{9,8},{10,11... | collective-permute-start | bytes 135176 | tf_op jit(solution)/shard_map/ppermute | solution.py:48
  4.7 6.7 %collective-permute-start.1 = (f32[88,128]{1,0:T(8,128)S(1)}, f32[88,128]{1,0:T(8,128)S(1)}, u32[]{:S(2)}, u32[]{:S(2)}) collective-permute-start(f32[88,128]{1,0:T(8,128)S(1)} %add.295), channel_id=1, source_target_pairs={{0,4},{1,5},{2,6},{3,7},{4,0},{5,1},{6,2},{7,3},{8,12},{9,13},{10,... | collective-permute-start | bytes 135176 | tf_op jit(solution)/shard_map/ppermute | solution.py:45
  8.0 5.3 %collective-permute-start.2 = (f32[88,128]{1,0:T(8,128)S(1)}, f32[88,128]{1,0:T(8,128)S(1)}, u32[]{:S(2)}, u32[]{:S(2)}) collective-permute-start(f32[88,128]{1,0:T(8,128)S(1)} %add.295), channel_id=1, source_target_pairs={{0,2},{1,3},{2,4},{3,5},{4,6},{5,7},{6,0},{7,1},{8,10},{9,11},{10,... | collective-permute-start | bytes 135176 | tf_op jit(solution)/shard_map/ppermute | solution.py:45
  8.7 4.6 %collective-permute-start.3 = (f32[88,128]{1,0:T(8,128)S(1)}, f32[88,128]{1,0:T(8,128)S(1)}, u32[]{:S(2)}, u32[]{:S(2)}) collective-permute-start(f32[88,128]{1,0:T(8,128)S(1)} %add.295), channel_id=1, source_target_pairs={{0,6},{1,7},{2,0},{3,1},{4,2},{5,3},{6,4},{7,5},{8,14},{9,15},{10,... | collective-permute-start | bytes 135176 | tf_op jit(solution)/shard_map/ppermute | solution.py:45
  13.3 2.6 %copy-start.1 = (f32[88,128]{1,0:T(8,128)}, f32[88,128]{1,0:T(8,128)S(1)}, u32[]{:S(2)}) copy-start(f32[88,128]{1,0:T(8,128)S(1)} %add_add_fusion) | copy-start | bytes 135172
  13.4 2.5 %copy-start.3 = (f32[128]{0:T(128)}, f32[128]{0:T(128)S(1)}, u32[]{:S(2)}) copy-start(f32[128]{0:T(128)S(1)} %slice_bitcast_fusion) | copy-start | bytes 1540
  14.8 34.3 %slice-start = ((s8[7340032]{0:T(1024)(128)(4,1)}), s8[3145728]{0:T(1024)(128)(4,1)S(1)}, s32[]{:S(2)}) async-start(s8[7340032]{0:T(1024)(128)(4,1)} %bitcast.133), calls=%async_computation.2 | async-start | bytes 6291456
  15.9 17.2 %all-to-all-start = ((bf16[16,24,512]{2,1,0:T(8,128)(2,1)}), bf16[16,24,512]{2,1,0:T(8,128)(2,1)S(1)}, u32[]{:S(2)}, u32[]{:S(2)}) async-start(bf16[16,24,512]{2,1,0:T(8,128)(2,1)} %bitcast.139), calls=%async_computation | async-start | bytes 786432 | tf_op jit(solution)/shard_map/all_to_all | solution.py:67
  33.0 14.0 %collective-permute-start.9 = (bf16[192,512]{1,0:T(8,128)(2,1)S(1)}, bf16[192,512]{1,0:T(8,128)(2,1)S(1)}, u32[]{:S(2)}, u32[]{:S(2)}) collective-permute-start(bf16[192,512]{1,0:T(8,128)(2,1)S(1)} %bitcast.144), channel_id=1, source_target_pairs={{0,6},{1,7},{2,0},{3,1},{4,2},{5,3},{6,4},{7,5},{8,14},{9,15},{10,... | collective-permute-start | bytes 589832 | tf_op jit(solution)/shard_map/ppermute | solution.py:45
  36.3 7.5 %collective-permute-start.4 = (bf16[192,512]{1,0:T(8,128)(2,1)S(1)}, bf16[192,512]{1,0:T(8,128)(2,1)S(1)}, u32[]{:S(2)}, u32[]{:S(2)}) collective-permute-start(bf16[192,512]{1,0:T(8,128)(2,1)S(1)} %bitcast.145), channel_id=1, source_target_pairs={{0,2},{1,3},{2,4},{3,5},{4,6},{5,7},{6,0},{7,1},{8,10},{9,11},{10,... | collective-permute-start | bytes 589832 | tf_op jit(solution)/shard_map/ppermute | solution.py:45
  36.3 7.5 %collective-permute-start.6 = (bf16[192,512]{1,0:T(8,128)(2,1)S(1)}, bf16[192,512]{1,0:T(8,128)(2,1)S(1)}, u32[]{:S(2)}, u32[]{:S(2)}) collective-permute-start(bf16[192,512]{1,0:T(8,128)(2,1)S(1)} %bitcast.142), channel_id=1, source_target_pairs={{0,6},{1,7},{2,0},{3,1},{4,2},{5,3},{6,4},{7,5},{8,14},{9,15},{10,... | collective-permute-start | bytes 589832 | tf_op jit(solution)/shard_map/ppermute | solution.py:45
  39.6 7.5 %collective-permute-start.8 = (bf16[192,512]{1,0:T(8,128)(2,1)S(1)}, bf16[192,512]{1,0:T(8,128)(2,1)S(1)}, u32[]{:S(2)}, u32[]{:S(2)}) collective-permute-start(bf16[192,512]{1,0:T(8,128)(2,1)S(1)} %bitcast.143), channel_id=1, source_target_pairs={{0,2},{1,3},{2,4},{3,5},{4,6},{5,7},{6,0},{7,1},{8,10},{9,11},{10,... | collective-permute-start | bytes 589832 | tf_op jit(solution)/shard_map/ppermute | solution.py:45
  39.6 7.6 %collective-permute-start.10 = (bf16[384,512]{1,0:T(8,128)(2,1)S(1)}, bf16[384,512]{1,0:T(8,128)(2,1)S(1)}, u32[]{:S(2)}, u32[]{:S(2)}) collective-permute-start(bf16[384,512]{1,0:T(8,128)(2,1)S(1)} %bitcast.135), channel_id=1, source_target_pairs={{0,1},{1,0},{2,3},{3,2},{4,5},{5,4},{6,7},{7,6},{8,9},{9,8},{10,11... | collective-permute-start | bytes 1179656 | tf_op jit(solution)/shard_map/ppermute | solution.py:48
  41.3 7.8 %slice-start.1 = ((s8[7340032]{0:T(1024)(128)(4,1)}), s8[4194304]{0:T(1024)(128)(4,1)S(1)}, s32[]{:S(2)}) async-start(s8[7340032]{0:T(1024)(128)(4,1)} %bitcast.133), calls=%async_computation.3 | async-start | bytes 8388608
  43.8 11.5 %collective-permute-start.5 = (bf16[192,512]{1,0:T(8,128)(2,1)S(1)}, bf16[192,512]{1,0:T(8,128)(2,1)S(1)}, u32[]{:S(2)}, u32[]{:S(2)}) collective-permute-start(bf16[192,512]{1,0:T(8,128)(2,1)S(1)} %collective-permute-done.4), channel_id=1, source_target_pairs={{0,2},{1,3},{2,4},{3,5},{4,6},{5,7},{6,0},{7,1},{8,10},{9,11},{10,... | collective-permute-start | bytes 589832 | tf_op jit(solution)/shard_map/ppermute | solution.py:45
  43.8 11.5 %collective-permute-start.7 = (bf16[192,512]{1,0:T(8,128)(2,1)S(1)}, bf16[192,512]{1,0:T(8,128)(2,1)S(1)}, u32[]{:S(2)}, u32[]{:S(2)}) collective-permute-start(bf16[192,512]{1,0:T(8,128)(2,1)S(1)} %collective-permute-done.6), channel_id=1, source_target_pairs={{0,6},{1,7},{2,0},{3,1},{4,2},{5,3},{6,4},{7,5},{8,14},{9,15},{10,... | collective-permute-start | bytes 589832 | tf_op jit(solution)/shard_map/ppermute | solution.py:45
  47.1 3.4 %copy-start = (bf16[1,4096,896]{2,1,0:T(8,128)(2,1)S(1)}, bf16[1,4096,896]{2,1,0:T(8,128)(2,1)}, u32[]{:S(2)}) copy-start(bf16[1,4096,896]{2,1,0:T(8,128)(2,1)} %param.20) | copy-start | bytes 22020100
  49.7 4.4 %collective-permute-start.11 = (bf16[384,512]{1,0:T(8,128)(2,1)S(1)}, bf16[384,512]{1,0:T(8,128)(2,1)S(1)}, u32[]{:S(2)}, u32[]{:S(2)}) collective-permute-start(bf16[384,512]{1,0:T(8,128)(2,1)S(1)} %pad_maximum_fusion), channel_id=1, source_target_pairs={{0,1},{1,0},{2,3},{3,2},{4,5},{5,4},{6,7},{7,6},{8,9},{9,8},{10,11... | collective-permute-start | bytes 1179656 | tf_op jit(solution)/shard_map/ppermute | solution.py:48
  51.1 1.9 %collective-permute-start.12 = (bf16[384,512]{1,0:T(8,128)(2,1)S(1)}, bf16[384,512]{1,0:T(8,128)(2,1)S(1)}, u32[]{:S(2)}, u32[]{:S(2)}) collective-permute-start(bf16[384,512]{1,0:T(8,128)(2,1)S(1)} %pad_maximum_fusion.1), channel_id=1, source_target_pairs={{0,1},{1,0},{2,3},{3,2},{4,5},{5,4},{6,7},{7,6},{8,9},{9,8},{10,11... | collective-permute-start | bytes 1179656 | tf_op jit(solution)/shard_map/ppermute | solution.py:48
  55.4 2.1 %collective-permute-start.13 = (bf16[384,512]{1,0:T(8,128)(2,1)S(1)}, bf16[384,512]{1,0:T(8,128)(2,1)S(1)}, u32[]{:S(2)}, u32[]{:S(2)}) collective-permute-start(bf16[384,512]{1,0:T(8,128)(2,1)S(1)} %constant_dynamic-update-slice_fusion), channel_id=1, source_target_pairs={{0,1},{1,0},{2,3},{3,2},{4,5},{5,4},{6,7},{7,6},{8,9},{9,8},{10,11... | collective-permute-start | bytes 1179656 | tf_op jit(solution)/shard_map/ppermute | solution.py:48
  62.1 7.0 %collective-permute-start.15 = (bf16[384,512]{1,0:T(8,128)(2,1)S(1)}, bf16[384,512]{1,0:T(8,128)(2,1)S(1)}, u32[]{:S(2)}, u32[]{:S(2)}) collective-permute-start(bf16[384,512]{1,0:T(8,128)(2,1)S(1)} %convolution_convert_fusion.2), channel_id=1, source_target_pairs={{0,1},{1,0},{2,3},{3,2},{4,5},{5,4},{6,7},{7,6},{8,9},{9,8},{10,11... | collective-permute-start | bytes 1179656 | tf_op jit(solution)/shard_map/ppermute | solution.py:48
  62.5 2.0 %collective-permute-start.16 = (bf16[384,512]{1,0:T(8,128)(2,1)S(1)}, bf16[384,512]{1,0:T(8,128)(2,1)S(1)}, u32[]{:S(2)}, u32[]{:S(2)}) collective-permute-start(bf16[384,512]{1,0:T(8,128)(2,1)S(1)} %convolution_convert_fusion.1), channel_id=1, source_target_pairs={{0,1},{1,0},{2,3},{3,2},{4,5},{5,4},{6,7},{7,6},{8,9},{9,8},{10,11... | collective-permute-start | bytes 1179656 | tf_op jit(solution)/shard_map/ppermute | solution.py:48
  63.3 2.0 %collective-permute-start.19 = (bf16[384,512]{1,0:T(8,128)(2,1)S(1)}, bf16[384,512]{1,0:T(8,128)(2,1)S(1)}, u32[]{:S(2)}, u32[]{:S(2)}) collective-permute-start(bf16[384,512]{1,0:T(8,128)(2,1)S(1)} %convolution_convert_fusion), channel_id=1, source_target_pairs={{0,1},{1,0},{2,3},{3,2},{4,5},{5,4},{6,7},{7,6},{8,9},{9,8},{10,11... | collective-permute-start | bytes 1179656 | tf_op jit(solution)/shard_map/ppermute | solution.py:48
  64.3 20.9 %collective-permute-start.14 = (bf16[384,512]{1,0:T(8,128)(2,1)S(1)}, bf16[384,512]{1,0:T(8,128)(2,1)S(1)}, u32[]{:S(2)}, u32[]{:S(2)}) collective-permute-start(bf16[384,512]{1,0:T(8,128)(2,1)S(1)} %convolution_convert_fusion.3), channel_id=1, source_target_pairs={{0,1},{1,0},{2,3},{3,2},{4,5},{5,4},{6,7},{7,6},{8,9},{9,8},{10,11... | collective-permute-start | bytes 1179656 | tf_op jit(solution)/shard_map/ppermute | solution.py:48
  65.1 8.6 %collective-permute-start.17 = (bf16[192,512]{1,0:T(8,128)(2,1)S(1)}, bf16[192,512]{1,0:T(8,128)(2,1)S(1)}, u32[]{:S(2)}, u32[]{:S(2)}) collective-permute-start(bf16[192,512]{1,0:T(8,128)(2,1)S(1)} %get-tuple-element.23), channel_id=1, source_target_pairs={{0,2},{1,3},{2,4},{3,5},{4,6},{5,7},{6,0},{7,1},{8,10},{9,11},{10,... | collective-permute-start | bytes 589832 | tf_op jit(solution)/shard_map/ppermute | solution.py:45
  65.8 15.7 %collective-permute-start.20 = (bf16[192,512]{1,0:T(8,128)(2,1)S(1)}, bf16[192,512]{1,0:T(8,128)(2,1)S(1)}, u32[]{:S(2)}, u32[]{:S(2)}) collective-permute-start(bf16[192,512]{1,0:T(8,128)(2,1)S(1)} %slice.116), channel_id=1, source_target_pairs={{0,6},{1,7},{2,0},{3,1},{4,2},{5,3},{6,4},{7,5},{8,14},{9,15},{10,... | collective-permute-start | bytes 589832 | tf_op jit(solution)/shard_map/ppermute | solution.py:45
  69.7 12.3 %collective-permute-start.21 = (bf16[192,512]{1,0:T(8,128)(2,1)S(1)}, bf16[192,512]{1,0:T(8,128)(2,1)S(1)}, u32[]{:S(2)}, u32[]{:S(2)}) collective-permute-start(bf16[192,512]{1,0:T(8,128)(2,1)S(1)} %slice.115), channel_id=1, source_target_pairs={{0,2},{1,3},{2,4},{3,5},{4,6},{5,7},{6,0},{7,1},{8,10},{9,11},{10,... | collective-permute-start | bytes 589832 | tf_op jit(solution)/shard_map/ppermute | solution.py:45
  69.8 7.9 %collective-permute-start.22 = (bf16[192,512]{1,0:T(8,128)(2,1)S(1)}, bf16[192,512]{1,0:T(8,128)(2,1)S(1)}, u32[]{:S(2)}, u32[]{:S(2)}) collective-permute-start(bf16[192,512]{1,0:T(8,128)(2,1)S(1)} %get-tuple-element.24), channel_id=1, source_target_pairs={{0,6},{1,7},{2,0},{3,1},{4,2},{5,3},{6,4},{7,5},{8,14},{9,15},{10,... | collective-permute-start | bytes 589832 | tf_op jit(solution)/shard_map/ppermute | solution.py:45
  73.8 8.2 %collective-permute-start.18 = (bf16[192,512]{1,0:T(8,128)(2,1)S(1)}, bf16[192,512]{1,0:T(8,128)(2,1)S(1)}, u32[]{:S(2)}, u32[]{:S(2)}) collective-permute-start(bf16[192,512]{1,0:T(8,128)(2,1)S(1)} %fusion.87), channel_id=1, source_target_pairs={{0,2},{1,3},{2,4},{3,5},{4,6},{5,7},{6,0},{7,1},{8,10},{9,11},{10,... | collective-permute-start | bytes 589832 | tf_op jit(solution)/shard_map/ppermute | solution.py:45
  77.8 7.4 %collective-permute-start.23 = (bf16[192,512]{1,0:T(8,128)(2,1)S(1)}, bf16[192,512]{1,0:T(8,128)(2,1)S(1)}, u32[]{:S(2)}, u32[]{:S(2)}) collective-permute-start(bf16[192,512]{1,0:T(8,128)(2,1)S(1)} %fusion.86), channel_id=1, source_target_pairs={{0,6},{1,7},{2,0},{3,1},{4,2},{5,3},{6,4},{7,5},{8,14},{9,15},{10,... | collective-permute-start | bytes 589832 | tf_op jit(solution)/shard_map/ppermute | solution.py:45
  86.6 13.1 %all-to-all-start.1 = ((bf16[16,24,512]{2,1,0:T(8,128)(2,1)}), bf16[16,24,512]{2,1,0:T(8,128)(2,1)S(1)}, u32[]{:S(2)}, u32[]{:S(2)}) async-start(bf16[16,24,512]{2,1,0:T(8,128)(2,1)} %bitcast.35), calls=%async_computation.1 | async-start | bytes 786432 | tf_op jit(solution)/shard_map/all_to_all | solution.py:135
  (2 other events, 4.4 us)
where the time goes:
time: 102 us; the launch traced here: 101 us
  starting transfers between devices  41 us (40%)
  waiting for transfers between devices  28.4 us (28%)
  matrix products  22.9 us (22%)
  other arithmetic  2.64 us (3%)
  local copies, waits for them, and re-layouts  2.59 us (3%)
  Pallas kernels  2.48 us (2%)
    ppermute x15, starting transfers between devices, along_y(): lax.ppermute(v, 'tensor', [(s, (s // 2 + k) % n_y * 2 + s % 2) for s in r...  26.8 us
    dot_general x24, matrix products, dot(): return jnp.dot(p, q, preferred_element_type=f32)  18.5 us
    ppermute x15, waiting for transfers between devices, along_y(): lax.ppermute(v, 'tensor', [(s, (s // 2 + k) % n_y * 2 + s % 2) for s in r...  10.6 us
    all_to_all x1, waiting for transfers between devices, on_device(): lax.all_to_all(reduced.astype(bf).reshape(-1, capacity, width), 'dp', spl...  8.99 us
    all_to_all x1, starting transfers between devices, on_device(): lax.all_to_all(sent.reshape(-1, capacity, width), 'dp', split_axis=0, con...  8.02 us
    all_to_all x1, waiting for transfers between devices, on_device(): lax.all_to_all(sent.reshape(-1, capacity, width), 'dp', split_axis=0, con...  7.97 us
    all_to_all x1, starting transfers between devices, on_device(): lax.all_to_all(reduced.astype(bf).reshape(-1, capacity, width), 'dp', spl...  3.98 us
    pallas_call x1, Pallas kernels, on_device(): pl.pallas_call(sums_kernel, out_shape=jax.ShapeDtypeStruct((rows + 24, ra...  2.48 us
  transfers between devices with their start and end apart: 26, of which 10 were waited for; matrix products, arithmetic and copies ran while one was open for 17% of the time, Pallas kernels for 0%

commit v1 on v0

v1 whole, which is shorter than its diff:
```python
import jax
import jax.numpy as jnp
from jax import lax
from jax.experimental import pallas as pl
from jax.experimental.pallas import tpu as pltpu
from jax.sharding import PartitionSpec as P

E = 8
HIGHEST = lax.Precision.HIGHEST


def dot32(a, b):
    return jnp.dot(a, b, precision=HIGHEST, preferred_element_type=jnp.float32)


def dot32_nt(a, b):
    return lax.dot_general(a, b, (((1,), (1,)), ((), ())), precision=HIGHEST, preferred_element_type=jnp.float32)


def sums_kernel(tokens, gain, mean, eraser_in, eraser_out, router_t, out, gained_out, eraser_out_copy):
    rows = tokens.shape[0]
    values = tokens[...].astype(jnp.float32)
    gained = values * gain[...]
    out[:rows] = dot32(gained, eraser_in[...])
    out[rows : rows + 8] = dot32(jnp.broadcast_to(mean[...], (8, mean.shape[1])), eraser_in[...])
    out[rows + 8 : rows + 16] = dot32(router_t[...], eraser_out[...])
    gained_out[...] = gained
    eraser_out_copy[...] = eraser_out[...]
    out[rows + 16 : rows + 24, :rows] = dot32_nt(router_t[...], gained)
    out[rows + 16 : rows + 24, rows : 2 * rows] = dot32_nt(jnp.ones((8, values.shape[1]), jnp.float32), values * values)


def on_device(tokens, norm_gain, eraser_mean, eraser_in, eraser_out, router, expert_ids, slots, w_gate, w_up, w_down):
    bf = jnp.bfloat16
    f32 = jnp.float32
    n_t = lax.axis_size("tensor")
    part_count = lax.axis_size("dp") // E
    rows, width = tokens.shape
    capacity = 3 * rows // 8
    full = width * n_t
    total = lax.axis_size("dp") * capacity
    rank = eraser_in.shape[1]
    t = lax.axis_index("tensor").astype(jnp.uint32)
    first = [(t ^ jnp.uint32(v)) * jnp.uint32(width) for v in range(n_t)]
    zero = t & jnp.uint32(0)
    tokens, zero, *first = lax.optimization_barrier((tokens, zero, *first))

    def swap_y(v, k):
        return lax.ppermute(v, "tensor", [(s, s ^ (2 * k)) for s in range(n_t)])

    def to_twin(v):
        return lax.ppermute(v, "tensor", [(s, s ^ 1) for s in range(n_t)])

    target = jnp.where(slots < capacity, expert_ids * capacity + slots, -1)
    place = jnp.arange(total, dtype=jnp.int32)
    place = (place // capacity // part_count) * capacity + place % capacity
    match = target.T[:, None, :] == place[None, :, None]
    placing = lax.optimization_barrier(jnp.any(match, axis=0).astype(bf))
    packed, gained, eraser_out = pl.pallas_call(
        sums_kernel,
        out_shape=[pltpu.VMEM((rows + 24, rank), f32), pltpu.VMEM((rows, width), f32), pltpu.VMEM((width, rank), f32)],
        out_specs=[pl.BlockSpec(memory_space=pltpu.VMEM)] * 3,
        name="sums",
    )(tokens, norm_gain[None, :], eraser_mean[None, :], eraser_in, eraser_out, router.T)
    packed = packed + to_twin(packed)
    sums = (packed + swap_y(packed, 2)) + (swap_y(packed, 1) + swap_y(packed, 3))
    inv_rms = lax.rsqrt(sums[rows + 16, rows : 2 * rows] / full + 1e-05)
    projected = inv_rms[:, None] * sums[:rows] - sums[rows : rows + 1]
    erased = (inv_rms[:, None] * gained - dot32_nt(projected, eraser_out)).astype(bf)
    sent = jnp.dot(placing, erased, preferred_element_type=f32).astype(bf)
    own = lax.all_to_all(sent.reshape(-1, capacity, width), "dp", split_axis=0, concat_axis=0, tiled=True)
    own = own.reshape(total, width)

    own, sums, inv_rms = lax.optimization_barrier((own, sums, inv_rms))

    mean_in = sums[rows : rows + 1]
    out_router_t = sums[rows + 8 : rows + 16]
    projected = inv_rms[:, None] * sums[:rows] - mean_in
    logits = inv_rms[:, None] * sums[rows + 16 : rows + 24, :rows].T - lax.dot_general(
        projected, out_router_t, (((1,), (1,)), ((), ())), precision=HIGHEST, preferred_element_type=f32
    )
    chosen = (expert_ids[:, :, None] == jnp.arange(E, dtype=jnp.int32)[None, None, :]).astype(f32)
    picked = jnp.sum(chosen * logits[:, None, :], axis=2)
    first_gate = jax.nn.sigmoid(picked[:, 0] - picked[:, 1])
    gate_pair = jnp.stack([first_gate, 1.0 - first_gate], axis=1)
    weights = jnp.sum((target[:, :, None] == place[None, None, :]).astype(f32) * gate_pair[:, :, None], axis=1)

    half = total // 2
    wg, wu, wd = w_gate[0], w_up[0], w_down[0]

    def rows_of(w, k, d):
        return lax.dynamic_slice(w, (first[2 * k + d], zero), (width, w.shape[1]))

    def cols_of(w, k, d):
        return lax.dynamic_slice(w, (zero, first[2 * k + d]), (w.shape[0], width))

    def dot(p, q):
        return jnp.dot(p, q, preferred_element_type=f32)

    def add_to(acc, *pieces):
        for piece, k, core in pieces:
            g = dot(piece, rows_of(wg, k, core))
            u = dot(piece, rows_of(wu, k, core))
            acc = (g, u) if acc is None else (acc[0] + g, acc[1] + u)
        return acc

    near1_b = swap_y(own[half:], 1)
    near3_a = swap_y(own[:half], 3)
    near1_a = swap_y(own[:half], 1)
    near3_b = swap_y(own[half:], 3)
    own2 = to_twin(own)
    acc = add_to(None, (own, 0, 0))
    acc = add_to(acc, (own2, 0, 1))
    far_a = swap_y(near3_a, 1)
    far_b = swap_y(near1_b, 3)
    near1 = jnp.concatenate([near1_a, near1_b], axis=0)
    near3 = jnp.concatenate([near3_a, near3_b], axis=0)
    near1, near3, acc = lax.optimization_barrier((near1, near3, acc))
    twin1 = to_twin(near1)
    twin3 = to_twin(near3)
    acc = add_to(acc, (near1, 1, 0), (near3, 3, 0), (twin1, 1, 1), (twin3, 3, 1))
    far_a, far_b, acc = lax.optimization_barrier((far_a, far_b, acc))
    far = jnp.concatenate([far_a, far_b], axis=0)
    far2 = to_twin(far)
    gate_act, up_act = add_to(acc, (far, 2, 0), (far2, 2, 1))
    hidden = (jax.nn.silu(gate_act) * up_act).astype(bf)

    def summed(k):
        other = dot(hidden, cols_of(wd, k, 1)).astype(bf)
        return dot(hidden, cols_of(wd, k, 0)) + to_twin(other).astype(f32)

    far = summed(2).astype(bf)
    got_a = swap_y(far[:half], 3)
    got_b = swap_y(far[half:], 1)
    to1 = summed(1)
    to3 = summed(3)
    from1_b = swap_y(to1[half:].astype(bf), 1)
    from3_a = swap_y(to3[:half].astype(bf), 3)
    mine = summed(0)
    from1_a = swap_y((to1[:half] + got_a.astype(f32)).astype(bf), 1)
    from3_b = swap_y((to3[half:] + got_b.astype(f32)).astype(bf), 3)
    reduced = mine + jnp.concatenate(
        [from1_a.astype(f32) + from3_a.astype(f32), from1_b.astype(f32) + from3_b.astype(f32)], axis=0
    )
    reduced, weights = lax.optimization_barrier((reduced.astype(bf), weights))
    returned = lax.all_to_all(
        reduced.reshape(-1, capacity, width), "dp", split_axis=0, concat_axis=0, tiled=True
    )
    mixed = jnp.dot(weights, returned.reshape(total, width).astype(f32), precision=HIGHEST, preferred_element_type=f32)
    return mixed.astype(bf)


def solution(mesh):
    in_specs = (
        P("dp", "tensor"),
        P("tensor"),
        P("tensor"),
        P("tensor", None),
        P("tensor", None),
        P("tensor", None),
        P("dp", None),
        P("dp", None),
        P("dp", None, "tensor"),
        P("dp", None, "tensor"),
        P("dp", "tensor", None),
    )

    return jax.shard_map(on_device, mesh=mesh, in_specs=in_specs, out_specs=P("dp", "tensor"), check_vma=False)
```

time: 102 us -> 101 us (level); the launches traced: 101 us -> 101 us
  blocking collectives: 0 us -> 29.7 us
  starting transfers between devices: 41 us -> 20.5 us
  waiting for transfers between devices: 28.4 us -> 23.1 us
  matrix products: 22.9 us -> 21.1 us
    all_to_all x0 -> x2, blocking collectives: none -> 29.7 us  [the longest x1 17.1 us: on_device(): lax.all_to_all(sent.reshape(-1, capacity, width), 'dp', split_axis=0, con...]
    all_to_all x2 -> x0, waiting for transfers between devices: 17 us -> none  [the longest x1 8.99 us: on_device(): lax.all_to_all(reduced.astype(bf).reshape(-1, capacity, width), 'dp', spl...]
    all_to_all x2 -> x0, starting transfers between devices: 12 us -> none  [the longest x1 8.02 us: on_device(): lax.all_to_all(sent.reshape(-1, capacity, width), 'dp', split_axis=0, con...]
    ppermute x15, waiting for transfers between devices: 10.6 us -> 22.5 us  [swap_y(): return lax.ppermute(v, 'tensor', [(s, s ^ 2 * k) for s in range(n_t)])]
    ppermute x15, starting transfers between devices: 26.8 us -> 18.3 us  [swap_y(): return lax.ppermute(v, 'tensor', [(s, s ^ 2 * k) for s in range(n_t)])]
    unnamed x17 -> x13, local copies, waits for them, and re-layouts: 2.47 us -> 2.29 us
  transfers between devices with their start and end apart: 26 -> 24, of which waited for: 10 -> 10; matrix products, arithmetic and copies ran while one was open for 17% -> 17% of each run, Pallas kernels for 0% -> 0%
where the time goes in v1:
time: 101 us
  blocking collectives  29.7 us (29%)
  waiting for transfers between devices  23.1 us (23%)
  matrix products  21.1 us (21%)
  starting transfers between devices  20.5 us (20%)
  local copies, waits for them, and re-layouts  2.41 us (2%)
  Pallas kernels  1.87 us (2%)
  other arithmetic  1.84 us (2%)
    ppermute x15, waiting for transfers between devices, swap_y(): return lax.ppermute(v, 'tensor', [(s, s ^ 2 * k) for s in range(n_t)])  22.5 us
    dot_general x24, matrix products, dot(): return jnp.dot(p, q, preferred_element_type=f32)  19.3 us
    ppermute x15, starting transfers between devices, swap_y(): return lax.ppermute(v, 'tensor', [(s, s ^ 2 * k) for s in range(n_t)])  18.3 us
    all_to_all x1, blocking collectives, on_device(): lax.all_to_all(sent.reshape(-1, capacity, width), 'dp', split_axis=0, con...  17.1 us
    all_to_all x1, blocking collectives, on_device(): lax.all_to_all(reduced.reshape(-1, capacity, width), 'dp', split_axis=0,...  12.7 us
    unnamed x13, local copies, waits for them, and re-layouts  2.29 us
    ppermute x9, starting transfers between devices, to_twin(): return lax.ppermute(v, 'tensor', [(s, s ^ 1) for s in range(n_t)])  2.19 us
  transfers between devices with their start and end apart: 24, of which 10 were waited for; matrix products, arithmetic and copies ran while one was open for 17% of the time, Pallas kernels for 0%

profile of v1, /device:TPU:0, one launch (start us, length us, event | category | flops | bytes accessed | tf_op | source)
XLA Modules:
  0.0 101.1 jit_solution(11464814126118467921)
XLA Ops:
  0.0 1.9 %sums.1 = (f32[88,128]{1,0:T(8,128)S(1)}, f32[64,512]{1,0:T(8,128)S(1)}, f32[512,128]{1,0:T(8,128)S(1)}) custom-call(bf16[64,512]{1,0:T(8,128)(2,1)} %tokens, f32[1,512]{1,0:T(1,128)} %bitcast.144, f32[1,512]{1,0:T(1,128)} %bitcast.145, f32[512,128]{1,0:T(8,128)} %eraser_in.1, f32[512,128]{1,0:T(8,128)} %eraser_out.1, f32[8,512]{1,0:T(8,128)} %bitcast.142), custom_call_target="tpu_custom_call" | custom-call | tf_op jit(solution)/shard_map/sums/pallas_call | solution.py:59
  1.9 0.7 compare_select_fusion
  3.1 3.4 %collective-permute-start.1 = (f32[88,128]{1,0:T(8,128)S(1)}, f32[88,128]{1,0:T(8,128)S(1)}, u32[]{:S(2)}, u32[]{:S(2)}) collective-permute-start(f32[88,128]{1,0:T(8,128)S(1)} %add.154), channel_id=1, source_target_pairs={{0,4},{1,5},{2,6},{3,7},{4,0},{5,1},{6,2},{7,3},{8,12},{9,13},{10,... | collective-permute-start | bytes 135176 | tf_op jit(solution)/shard_map/ppermute | solution.py:49
  7.7 1.1 %collective-permute-done.1 = f32[88,128]{1,0:T(8,128)S(1)} collective-permute-done((f32[88,128]{1,0:T(8,128)S(1)}, f32[88,128]{1,0:T(8,128)S(1)}, u32[]{:S(2)}, u32[]{:S(2)}) %collective-permute-start.1) | collective-permute-done | bytes 45088 | tf_op jit(solution)/shard_map/ppermute | solution.py:49
  8.7 1.8 %collective-permute-done.2 = f32[88,128]{1,0:T(8,128)S(1)} collective-permute-done((f32[88,128]{1,0:T(8,128)S(1)}, f32[88,128]{1,0:T(8,128)S(1)}, u32[]{:S(2)}, u32[]{:S(2)}) %collective-permute-start.2) | collective-permute-done | bytes 45088 | tf_op jit(solution)/shard_map/ppermute | solution.py:49
  10.5 1.9 %collective-permute-done.3 = f32[88,128]{1,0:T(8,128)S(1)} collective-permute-done((f32[88,128]{1,0:T(8,128)S(1)}, f32[88,128]{1,0:T(8,128)S(1)}, u32[]{:S(2)}, u32[]{:S(2)}) %collective-permute-start.3) | collective-permute-done | bytes 45088 | tf_op jit(solution)/shard_map/ppermute | solution.py:49
  13.3 17.1 %all_to_all.10 = bf16[16,24,512]{2,1,0:T(8,128)(2,1)S(1)} all-to-all(bf16[16,24,512]{2,1,0:T(8,128)(2,1)S(1)} %bitcast.138), channel_id=1, replica_groups=mesh['dp'=16,'tensor'=8] {'dp'}, dimensions={0} | all-to-all | bytes 786432 | tf_op jit(solution)/shard_map/all_to_all | solution.py:71
  30.4 0.7 collective-permute-start.9
  31.1 2.6 %collective-permute-start.4 = (bf16[192,512]{1,0:T(8,128)(2,1)S(1)}, bf16[192,512]{1,0:T(8,128)(2,1)S(1)}, u32[]{:S(2)}, u32[]{:S(2)}) collective-permute-start(bf16[192,512]{1,0:T(8,128)(2,1)S(1)} %get-tuple-element.60), channel_id=1, source_target_pairs={{0,6},{1,7},{2,4},{3,5},{4,2},{5,3},{6,0},{7,1},{8,14},{9,15},{10,... | collective-permute-start | bytes 589832 | tf_op jit(solution)/shard_map/ppermute | solution.py:49
  33.7 1.4 %collective-permute-start.8 = (bf16[192,512]{1,0:T(8,128)(2,1)S(1)}, bf16[192,512]{1,0:T(8,128)(2,1)S(1)}, u32[]{:S(2)}, u32[]{:S(2)}) collective-permute-start(bf16[192,512]{1,0:T(8,128)(2,1)S(1)} %get-tuple-element.60), channel_id=1, source_target_pairs={{0,2},{1,3},{2,0},{3,1},{4,6},{5,7},{6,4},{7,5},{8,10},{9,11},{10,... | collective-permute-start | bytes 589832 | tf_op jit(solution)/shard_map/ppermute | solution.py:49
  35.1 1.8 %fusion.57 = f32[384,896]{1,0:T(8,128)S(1)} fusion(bf16[384,512]{1,0:T(8,128)(2,1)S(1)} %bitcast.135, bf16[1,4096,896]{2,1,0:T(8,128)(2,1)} %param.20, u32[]{:T(128)S(6)} %mul.101), kind=kOutput, calls=%fused_computation.58 | convolution fusion | flops 352321536 | bytes 2686980 | tf_op jit(solution)/shard_map/dot_general | solution.py:98
  36.9 1.9 %fusion.60 = f32[384,896]{1,0:T(8,128)S(1)} fusion(bf16[384,512]{1,0:T(8,128)(2,1)S(1)} %bitcast.136, bf16[1,4096,896]{2,1,0:T(8,128)(2,1)} %param.19, u32[]{:T(128)S(6)} %mul.101), kind=kOutput, calls=%fused_computation.61 | convolution fusion | flops 352321536 | bytes 2686980 | tf_op jit(solution)/shard_map/dot_general | solution.py:98
  39.3 3.9 %collective-permute-done.4 = bf16[192,512]{1,0:T(8,128)(2,1)S(1)} collective-permute-done((bf16[192,512]{1,0:T(8,128)(2,1)S(1)}, bf16[192,512]{1,0:T(8,128)(2,1)S(1)}, u32[]{:S(2)}, u32[]{:S(2)}) %collective-permute-start.4) | collective-permute-done | bytes 196640 | tf_op jit(solution)/shard_map/ppermute | solution.py:49
  44.0 2.0 %convolution_add_fusion.4 = f32[384,896]{1,0:T(8,128)S(1)} fusion(f32[384,896]{1,0:T(8,128)S(1)} %fusion.57, bf16[384,512]{1,0:T(8,128)(2,1)S(1)} %collective-permute-done.10, bf16[1,4096,896]{2,1,0:T(8,128)(2,1)} %param.20, u32[]{:T(128)S(6)} %mul.102), kind=kOutput, calls=%fused_computation.4 | convolution fusion | flops 352665600 | bytes 4063236 | tf_op jit(solution)/shard_map/dot_general | solution.py:98
  52.5 0.8 collective-permute-start.13
  56.7 1.2 %slice-done.3 = s8[3145728]{0:T(1024)(128)(4,1)S(1)} async-done(((s8[7340032]{0:T(1024)(128)(4,1)}), s8[3145728]{0:T(1024)(128)(4,1)S(1)}, s32[]{:S(2)}) %slice-start.3) | async-done | bytes 3145752
  57.9 0.7 convolution_convert_fusion.2
  58.6 0.7 convolution_convert_fusion.1
  59.9 0.7 convolution_convert_fusion
  61.1 0.7 convolution_convert_fusion.3
  62.0 0.7 fusion.15
  62.8 2.7 %collective-permute-start.17 = (bf16[192,512]{1,0:T(8,128)(2,1)S(1)}, bf16[192,512]{1,0:T(8,128)(2,1)S(1)}, u32[]{:S(2)}, u32[]{:S(2)}) collective-permute-start(bf16[192,512]{1,0:T(8,128)(2,1)S(1)} %get-tuple-element.57), channel_id=1, source_target_pairs={{0,6},{1,7},{2,4},{3,5},{4,2},{5,3},{6,0},{7,1},{8,14},{9,15},{10,... | collective-permute-start | bytes 589832 | tf_op jit(solution)/shard_map/ppermute | solution.py:49
  66.2 0.7 collective-permute-start.20
  66.9 0.7 fusion.21
  67.9 1.8 %collective-permute-start.22 = (bf16[192,512]{1,0:T(8,128)(2,1)S(1)}, bf16[192,512]{1,0:T(8,128)(2,1)S(1)}, u32[]{:S(2)}, u32[]{:S(2)}) collective-permute-start(bf16[192,512]{1,0:T(8,128)(2,1)S(1)} %get-tuple-element.58), channel_id=1, source_target_pairs={{0,2},{1,3},{2,0},{3,1},{4,6},{5,7},{6,4},{7,5},{8,10},{9,11},{10,... | collective-permute-start | bytes 589832 | tf_op jit(solution)/shard_map/ppermute | solution.py:49
  69.7 2.1 %collective-permute-done.17 = bf16[192,512]{1,0:T(8,128)(2,1)S(1)} collective-permute-done((bf16[192,512]{1,0:T(8,128)(2,1)S(1)}, bf16[192,512]{1,0:T(8,128)(2,1)S(1)}, u32[]{:S(2)}, u32[]{:S(2)}) %collective-permute-start.17) | collective-permute-done | bytes 196640 | tf_op jit(solution)/shard_map/ppermute | solution.py:49
  72.2 7.5 %collective-permute-done.22 = bf16[192,512]{1,0:T(8,128)(2,1)S(1)} collective-permute-done((bf16[192,512]{1,0:T(8,128)(2,1)S(1)}, bf16[192,512]{1,0:T(8,128)(2,1)S(1)}, u32[]{:S(2)}, u32[]{:S(2)}) %collective-permute-start.22) | collective-permute-done | bytes 196640 | tf_op jit(solution)/shard_map/ppermute | solution.py:49
  79.7 2.7 %collective-permute-start.23 = (bf16[192,512]{1,0:T(8,128)(2,1)S(1)}, bf16[192,512]{1,0:T(8,128)(2,1)S(1)}, u32[]{:S(2)}, u32[]{:S(2)}) collective-permute-start(bf16[192,512]{1,0:T(8,128)(2,1)S(1)} %fusion.86), channel_id=1, source_target_pairs={{0,6},{1,7},{2,4},{3,5},{4,2},{5,3},{6,0},{7,1},{8,14},{9,15},{10,... | collective-permute-start | bytes 589832 | tf_op jit(solution)/shard_map/ppermute | solution.py:49
  82.8 3.9 %collective-permute-done.23 = bf16[192,512]{1,0:T(8,128)(2,1)S(1)} collective-permute-done((bf16[192,512]{1,0:T(8,128)(2,1)S(1)}, bf16[192,512]{1,0:T(8,128)(2,1)S(1)}, u32[]{:S(2)}, u32[]{:S(2)}) %collective-permute-start.23) | collective-permute-done | bytes 196640 | tf_op jit(solution)/shard_map/ppermute | solution.py:49
  86.8 0.7 fusion.33
  87.5 12.7 %all_to_all.11 = bf16[16,24,512]{2,1,0:T(8,128)(2,1)S(1)} all-to-all(bf16[16,24,512]{2,1,0:T(8,128)(2,1)S(1)} %bitcast.141), channel_id=1, replica_groups=mesh['dp'=16,'tensor'=8] {'dp'}, dimensions={0} | all-to-all | bytes 786432 | tf_op jit(solution)/shard_map/all_to_all | solution.py:146
  100.1 1.0 convolution_convert_fusion.5
  (87 shorter events, 16.7 us)
Async XLA Ops:
  1.9 1.2 %collective-permute-start = (f32[88,128]{1,0:T(8,128)S(1)}, f32[88,128]{1,0:T(8,128)S(1)}, u32[]{:S(2)}, u32[]{:S(2)}) collective-permute-start(f32[88,128]{1,0:T(8,128)S(1)} %get-tuple-element.31), channel_id=1, source_target_pairs={{0,1},{1,0},{2,3},{3,2},{4,5},{5,4},{6,7},{7,6},{8,9},{9,8},{10,11... | collective-permute-start | bytes 135176 | tf_op jit(solution)/shard_map/ppermute | solution.py:52
  3.1 5.6 %collective-permute-start.1 = (f32[88,128]{1,0:T(8,128)S(1)}, f32[88,128]{1,0:T(8,128)S(1)}, u32[]{:S(2)}, u32[]{:S(2)}) collective-permute-start(f32[88,128]{1,0:T(8,128)S(1)} %add.154), channel_id=1, source_target_pairs={{0,4},{1,5},{2,6},{3,7},{4,0},{5,1},{6,2},{7,3},{8,12},{9,13},{10,... | collective-permute-start | bytes 135176 | tf_op jit(solution)/shard_map/ppermute | solution.py:49
  6.5 4.0 %collective-permute-start.2 = (f32[88,128]{1,0:T(8,128)S(1)}, f32[88,128]{1,0:T(8,128)S(1)}, u32[]{:S(2)}, u32[]{:S(2)}) collective-permute-start(f32[88,128]{1,0:T(8,128)S(1)} %add.154), channel_id=1, source_target_pairs={{0,2},{1,3},{2,0},{3,1},{4,6},{5,7},{6,4},{7,5},{8,10},{9,11},{10,... | collective-permute-start | bytes 135176 | tf_op jit(solution)/shard_map/ppermute | solution.py:49
  7.2 5.3 %collective-permute-start.3 = (f32[88,128]{1,0:T(8,128)S(1)}, f32[88,128]{1,0:T(8,128)S(1)}, u32[]{:S(2)}, u32[]{:S(2)}) collective-permute-start(f32[88,128]{1,0:T(8,128)S(1)} %add.154), channel_id=1, source_target_pairs={{0,6},{1,7},{2,4},{3,5},{4,2},{5,3},{6,0},{7,1},{8,14},{9,15},{10,... | collective-permute-start | bytes 135176 | tf_op jit(solution)/shard_map/ppermute | solution.py:49
  13.0 33.0 %slice-start = ((s8[7340032]{0:T(1024)(128)(4,1)}), s8[4194304]{0:T(1024)(128)(4,1)S(1)}, s32[]{:S(2)}) async-start(s8[7340032]{0:T(1024)(128)(4,1)} %bitcast.131), calls=%async_computation.2 | async-start | bytes 8388608
  30.3 13.6 %collective-permute-start.10 = (bf16[384,512]{1,0:T(8,128)(2,1)S(1)}, bf16[384,512]{1,0:T(8,128)(2,1)S(1)}, u32[]{:S(2)}, u32[]{:S(2)}) collective-permute-start(bf16[384,512]{1,0:T(8,128)(2,1)S(1)} %bitcast.133), channel_id=1, source_target_pairs={{0,1},{1,0},{2,3},{3,2},{4,5},{5,4},{6,7},{7,6},{8,9},{9,8},{10,11... | collective-permute-start | bytes 1179656 | tf_op jit(solution)/shard_map/ppermute | solution.py:52
  30.4 13.5 %collective-permute-start.9 = (bf16[192,512]{1,0:T(8,128)(2,1)S(1)}, bf16[192,512]{1,0:T(8,128)(2,1)S(1)}, u32[]{:S(2)}, u32[]{:S(2)}) collective-permute-start(bf16[192,512]{1,0:T(8,128)(2,1)S(1)} %get-tuple-element.59), channel_id=1, source_target_pairs={{0,6},{1,7},{2,4},{3,5},{4,2},{5,3},{6,0},{7,1},{8,14},{9,15},{10,... | collective-permute-start | bytes 589832 | tf_op jit(solution)/shard_map/ppermute | solution.py:49
  31.1 12.1 %collective-permute-start.6 = (bf16[192,512]{1,0:T(8,128)(2,1)S(1)}, bf16[192,512]{1,0:T(8,128)(2,1)S(1)}, u32[]{:S(2)}, u32[]{:S(2)}) collective-permute-start(bf16[192,512]{1,0:T(8,128)(2,1)S(1)} %get-tuple-element.59), channel_id=1, source_target_pairs={{0,2},{1,3},{2,0},{3,1},{4,6},{5,7},{6,4},{7,5},{8,10},{9,11},{10,... | collective-permute-start | bytes 589832 | tf_op jit(solution)/shard_map/ppermute | solution.py:49
  31.1 12.1 %collective-permute-start.4 = (bf16[192,512]{1,0:T(8,128)(2,1)S(1)}, bf16[192,512]{1,0:T(8,128)(2,1)S(1)}, u32[]{:S(2)}, u32[]{:S(2)}) collective-permute-start(bf16[192,512]{1,0:T(8,128)(2,1)S(1)} %get-tuple-element.60), channel_id=1, source_target_pairs={{0,6},{1,7},{2,4},{3,5},{4,2},{5,3},{6,0},{7,1},{8,14},{9,15},{10,... | collective-permute-start | bytes 589832 | tf_op jit(solution)/shard_map/ppermute | solution.py:49
  33.7 10.2 %collective-permute-start.8 = (bf16[192,512]{1,0:T(8,128)(2,1)S(1)}, bf16[192,512]{1,0:T(8,128)(2,1)S(1)}, u32[]{:S(2)}, u32[]{:S(2)}) collective-permute-start(bf16[192,512]{1,0:T(8,128)(2,1)S(1)} %get-tuple-element.60), channel_id=1, source_target_pairs={{0,2},{1,3},{2,0},{3,1},{4,6},{5,7},{6,4},{7,5},{8,10},{9,11},{10,... | collective-permute-start | bytes 589832 | tf_op jit(solution)/shard_map/ppermute | solution.py:49
  35.1 4.0 %copy-start.1 = (s32[64,2]{0,1:T(2,128)S(1)}, s32[64,2]{0,1:T(2,128)}, u32[]{:S(2)}) copy-start(s32[64,2]{0,1:T(2,128)} %param.17) | copy-start | bytes 1540
  36.9 9.0 %slice-start.1 = ((s8[7340032]{0:T(1024)(128)(4,1)}), s8[3145728]{0:T(1024)(128)(4,1)S(1)}, s32[]{:S(2)}) async-start(s8[7340032]{0:T(1024)(128)(4,1)} %bitcast.131), calls=%async_computation.3 | async-start | bytes 6291456
  43.2 9.2 %collective-permute-start.5 = (bf16[192,512]{1,0:T(8,128)(2,1)S(1)}, bf16[192,512]{1,0:T(8,128)(2,1)S(1)}, u32[]{:S(2)}, u32[]{:S(2)}) collective-permute-start(bf16[192,512]{1,0:T(8,128)(2,1)S(1)} %collective-permute-done.4), channel_id=1, source_target_pairs={{0,2},{1,3},{2,0},{3,1},{4,6},{5,7},{6,4},{7,5},{8,10},{9,11},{10,... | collective-permute-start | bytes 589832 | tf_op jit(solution)/shard_map/ppermute | solution.py:49
  43.2 9.2 %collective-permute-start.7 = (bf16[192,512]{1,0:T(8,128)(2,1)S(1)}, bf16[192,512]{1,0:T(8,128)(2,1)S(1)}, u32[]{:S(2)}, u32[]{:S(2)}) collective-permute-start(bf16[192,512]{1,0:T(8,128)(2,1)S(1)} %collective-permute-done.6), channel_id=1, source_target_pairs={{0,6},{1,7},{2,4},{3,5},{4,2},{5,3},{6,0},{7,1},{8,14},{9,15},{10,... | collective-permute-start | bytes 589832 | tf_op jit(solution)/shard_map/ppermute | solution.py:49
  43.9 3.4 %copy-start = (bf16[1,4096,896]{2,1,0:T(8,128)(2,1)S(1)}, bf16[1,4096,896]{2,1,0:T(8,128)(2,1)}, u32[]{:S(2)}) copy-start(bf16[1,4096,896]{2,1,0:T(8,128)(2,1)} %param.20) | copy-start | bytes 22020100
  46.6 4.5 %collective-permute-start.11 = (bf16[384,512]{1,0:T(8,128)(2,1)S(1)}, bf16[384,512]{1,0:T(8,128)(2,1)S(1)}, u32[]{:S(2)}, u32[]{:S(2)}) collective-permute-start(bf16[384,512]{1,0:T(8,128)(2,1)S(1)} %pad_maximum_fusion), channel_id=1, source_target_pairs={{0,1},{1,0},{2,3},{3,2},{4,5},{5,4},{6,7},{7,6},{8,9},{9,8},{10,11... | collective-permute-start | bytes 1179656 | tf_op jit(solution)/shard_map/ppermute | solution.py:52
  47.9 2.0 %collective-permute-start.12 = (bf16[384,512]{1,0:T(8,128)(2,1)S(1)}, bf16[384,512]{1,0:T(8,128)(2,1)S(1)}, u32[]{:S(2)}, u32[]{:S(2)}) collective-permute-start(bf16[384,512]{1,0:T(8,128)(2,1)S(1)} %pad_maximum_fusion.1), channel_id=1, source_target_pairs={{0,1},{1,0},{2,3},{3,2},{4,5},{5,4},{6,7},{7,6},{8,9},{9,8},{10,11... | collective-permute-start | bytes 1179656 | tf_op jit(solution)/shard_map/ppermute | solution.py:52
  52.5 2.1 %collective-permute-start.13 = (bf16[384,512]{1,0:T(8,128)(2,1)S(1)}, bf16[384,512]{1,0:T(8,128)(2,1)S(1)}, u32[]{:S(2)}, u32[]{:S(2)}) collective-permute-start(bf16[384,512]{1,0:T(8,128)(2,1)S(1)} %constant_dynamic-update-slice_fusion), channel_id=1, source_target_pairs={{0,1},{1,0},{2,3},{3,2},{4,5},{5,4},{6,7},{7,6},{8,9},{9,8},{10,11... | collective-permute-start | bytes 1179656 | tf_op jit(solution)/shard_map/ppermute | solution.py:52
  54.6 2.2 %slice-start.2 = ((s8[7340032]{0:T(1024)(128)(4,1)}), s8[4194304]{0:T(1024)(128)(4,1)S(1)}, s32[]{:S(2)}) async-start(s8[7340032]{0:T(1024)(128)(4,1)} %bitcast.139), calls=%async_computation.4 | async-start | bytes 8388608
  55.8 2.1 %slice-start.3 = ((s8[7340032]{0:T(1024)(128)(4,1)}), s8[3145728]{0:T(1024)(128)(4,1)S(1)}, s32[]{:S(2)}) async-start(s8[7340032]{0:T(1024)(128)(4,1)} %bitcast.139), calls=%async_computation.5 | async-start | bytes 6291456
  59.3 7.5 %collective-permute-start.15 = (bf16[384,512]{1,0:T(8,128)(2,1)S(1)}, bf16[384,512]{1,0:T(8,128)(2,1)S(1)}, u32[]{:S(2)}, u32[]{:S(2)}) collective-permute-start(bf16[384,512]{1,0:T(8,128)(2,1)S(1)} %convolution_convert_fusion.2), channel_id=1, source_target_pairs={{0,1},{1,0},{2,3},{3,2},{4,5},{5,4},{6,7},{7,6},{8,9},{9,8},{10,11... | collective-permute-start | bytes 1179656 | tf_op jit(solution)/shard_map/ppermute | solution.py:52
  59.8 2.2 %collective-permute-start.16 = (bf16[384,512]{1,0:T(8,128)(2,1)S(1)}, bf16[384,512]{1,0:T(8,128)(2,1)S(1)}, u32[]{:S(2)}, u32[]{:S(2)}) collective-permute-start(bf16[384,512]{1,0:T(8,128)(2,1)S(1)} %convolution_convert_fusion.1), channel_id=1, source_target_pairs={{0,1},{1,0},{2,3},{3,2},{4,5},{5,4},{6,7},{7,6},{8,9},{9,8},{10,11... | collective-permute-start | bytes 1179656 | tf_op jit(solution)/shard_map/ppermute | solution.py:52
  60.6 4.8 %collective-permute-start.19 = (bf16[384,512]{1,0:T(8,128)(2,1)S(1)}, bf16[384,512]{1,0:T(8,128)(2,1)S(1)}, u32[]{:S(2)}, u32[]{:S(2)}) collective-permute-start(bf16[384,512]{1,0:T(8,128)(2,1)S(1)} %convolution_convert_fusion), channel_id=1, source_target_pairs={{0,1},{1,0},{2,3},{3,2},{4,5},{5,4},{6,7},{7,6},{8,9},{9,8},{10,11... | collective-permute-start | bytes 1179656 | tf_op jit(solution)/shard_map/ppermute | solution.py:52
  61.8 25.0 %collective-permute-start.14 = (bf16[384,512]{1,0:T(8,128)(2,1)S(1)}, bf16[384,512]{1,0:T(8,128)(2,1)S(1)}, u32[]{:S(2)}, u32[]{:S(2)}) collective-permute-start(bf16[384,512]{1,0:T(8,128)(2,1)S(1)} %convolution_convert_fusion.3), channel_id=1, source_target_pairs={{0,1},{1,0},{2,3},{3,2},{4,5},{5,4},{6,7},{7,6},{8,9},{9,8},{10,11... | collective-permute-start | bytes 1179656 | tf_op jit(solution)/shard_map/ppermute | solution.py:52
  62.8 9.1 %collective-permute-start.17 = (bf16[192,512]{1,0:T(8,128)(2,1)S(1)}, bf16[192,512]{1,0:T(8,128)(2,1)S(1)}, u32[]{:S(2)}, u32[]{:S(2)}) collective-permute-start(bf16[192,512]{1,0:T(8,128)(2,1)S(1)} %get-tuple-element.57), channel_id=1, source_target_pairs={{0,6},{1,7},{2,4},{3,5},{4,2},{5,3},{6,0},{7,1},{8,14},{9,15},{10,... | collective-permute-start | bytes 589832 | tf_op jit(solution)/shard_map/ppermute | solution.py:49
  66.2 16.3 %collective-permute-start.20 = (bf16[192,512]{1,0:T(8,128)(2,1)S(1)}, bf16[192,512]{1,0:T(8,128)(2,1)S(1)}, u32[]{:S(2)}, u32[]{:S(2)}) collective-permute-start(bf16[192,512]{1,0:T(8,128)(2,1)S(1)} %slice.112), channel_id=1, source_target_pairs={{0,6},{1,7},{2,4},{3,5},{4,2},{5,3},{6,0},{7,1},{8,14},{9,15},{10,... | collective-permute-start | bytes 589832 | tf_op jit(solution)/shard_map/ppermute | solution.py:49
  67.6 15.2 %collective-permute-start.21 = (bf16[192,512]{1,0:T(8,128)(2,1)S(1)}, bf16[192,512]{1,0:T(8,128)(2,1)S(1)}, u32[]{:S(2)}, u32[]{:S(2)}) collective-permute-start(bf16[192,512]{1,0:T(8,128)(2,1)S(1)} %slice.111), channel_id=1, source_target_pairs={{0,2},{1,3},{2,0},{3,1},{4,6},{5,7},{6,4},{7,5},{8,10},{9,11},{10,... | collective-permute-start | bytes 589832 | tf_op jit(solution)/shard_map/ppermute | solution.py:49
  67.9 11.8 %collective-permute-start.22 = (bf16[192,512]{1,0:T(8,128)(2,1)S(1)}, bf16[192,512]{1,0:T(8,128)(2,1)S(1)}, u32[]{:S(2)}, u32[]{:S(2)}) collective-permute-start(bf16[192,512]{1,0:T(8,128)(2,1)S(1)} %get-tuple-element.58), channel_id=1, source_target_pairs={{0,2},{1,3},{2,0},{3,1},{4,6},{5,7},{6,4},{7,5},{8,10},{9,11},{10,... | collective-permute-start | bytes 589832 | tf_op jit(solution)/shard_map/ppermute | solution.py:49
  71.9 10.9 %collective-permute-start.18 = (bf16[192,512]{1,0:T(8,128)(2,1)S(1)}, bf16[192,512]{1,0:T(8,128)(2,1)S(1)}, u32[]{:S(2)}, u32[]{:S(2)}) collective-permute-start(bf16[192,512]{1,0:T(8,128)(2,1)S(1)} %fusion.87), channel_id=1, source_target_pairs={{0,2},{1,3},{2,0},{3,1},{4,6},{5,7},{6,4},{7,5},{8,10},{9,11},{10,... | collective-permute-start | bytes 589832 | tf_op jit(solution)/shard_map/ppermute | solution.py:49
  79.7 7.0 %collective-permute-start.23 = (bf16[192,512]{1,0:T(8,128)(2,1)S(1)}, bf16[192,512]{1,0:T(8,128)(2,1)S(1)}, u32[]{:S(2)}, u32[]{:S(2)}) collective-permute-start(bf16[192,512]{1,0:T(8,128)(2,1)S(1)} %fusion.86), channel_id=1, source_target_pairs={{0,6},{1,7},{2,4},{3,5},{4,2},{5,3},{6,0},{7,1},{8,14},{9,15},{10,... | collective-permute-start | bytes 589832 | tf_op jit(solution)/shard_map/ppermute | solution.py:49

commit v2 on v1

--- a/solution.py
+++ b/solution.py
@@ -28,6 +28,20 @@
     eraser_out_copy[...] = eraser_out[...]
     out[rows + 16 : rows + 24, :rows] = dot32_nt(router_t[...], gained)
     out[rows + 16 : rows + 24, rows : 2 * rows] = dot32_nt(jnp.ones((8, values.shape[1]), jnp.float32), values * values)
+
+
+def load_kernel(near_first, far_first, gate, up, down, gate_rows, up_rows, down_cols, sems):
+    near = pl.multiple_of(near_first[0], gate_rows.shape[0])
+    far = pl.multiple_of(far_first[0], down_cols.shape[1])
+    copies = (
+        pltpu.make_async_copy(gate.at[0, pl.ds(near, gate_rows.shape[0])], gate_rows, sems.at[0]),
+        pltpu.make_async_copy(up.at[0, pl.ds(near, up_rows.shape[0])], up_rows, sems.at[1]),
+        pltpu.make_async_copy(down.at[0, :, pl.ds(far, down_cols.shape[1])], down_cols, sems.at[2]),
+    )
+    for copy in copies:
+        copy.start()
+    for copy in copies:
+        copy.wait()
 
 
 def on_device(tokens, norm_gain, eraser_mean, eraser_in, eraser_out, router, expert_ids, slots, w_gate, w_up, w_down):
@@ -43,7 +57,14 @@
     t = lax.axis_index("tensor").astype(jnp.uint32)
     first = [(t ^ jnp.uint32(v)) * jnp.uint32(width) for v in range(n_t)]
     zero = t & jnp.uint32(0)
-    tokens, zero, *first = lax.optimization_barrier((tokens, zero, *first))
+    core_rows = (t & jnp.uint32(1)) * jnp.uint32(width)
+    twin_rows = jnp.uint32(width) - core_rows
+    chip = (t >> jnp.uint32(1)).astype(jnp.int32)
+    pair_first = (chip * (2 * width)).reshape(1)
+    far_first = ((chip ^ 2) * (2 * width)).reshape(1)
+    tokens, zero, core_rows, twin_rows, pair_first, far_first, *first = lax.optimization_barrier(
+        (tokens, zero, core_rows, twin_rows, pair_first, far_first, *first)
+    )
 
     def swap_y(v, k):
         return lax.ppermute(v, "tensor", [(s, s ^ (2 * k)) for s in range(n_t)])
@@ -62,6 +83,22 @@
         out_specs=[pl.BlockSpec(memory_space=pltpu.VMEM)] * 3,
         name="sums",
     )(tokens, norm_gain[None, :], eraser_mean[None, :], eraser_in, eraser_out, router.T)
+    pair_shapes = [(2 * width, w_gate.shape[2])] * 2 + [(w_down.shape[1], 2 * width)]
+    pair_gate, pair_up, far_down = pl.pallas_call(
+        load_kernel,
+        in_specs=[
+            pl.BlockSpec(memory_space=pltpu.SMEM),
+            pl.BlockSpec(memory_space=pltpu.SMEM),
+            pl.BlockSpec(memory_space=pltpu.HBM),
+            pl.BlockSpec(memory_space=pltpu.HBM),
+            pl.BlockSpec(memory_space=pltpu.HBM),
+        ],
+        out_shape=[pltpu.VMEM(shape, bf) for shape in pair_shapes],
+        out_specs=[pl.BlockSpec(memory_space=pltpu.VMEM)] * 3,
+        scratch_shapes=[pltpu.SemaphoreType.DMA((3,))],
+        compiler_params=pltpu.CompilerParams(vmem_limit_bytes=56 << 20),
+        name="load",
+    )(pair_first, far_first, w_gate, w_up, w_down)
     packed = packed + to_twin(packed)
     sums = (packed + swap_y(packed, 2)) + (swap_y(packed, 1) + swap_y(packed, 3))
     inv_rms = lax.rsqrt(sums[rows + 16, rows : 2 * rows] / full + 1e-05)
@@ -94,6 +131,9 @@
     def cols_of(w, k, d):
         return lax.dynamic_slice(w, (zero, first[2 * k + d]), (w.shape[0], width))
 
+    def far_cols(begin):
+        return lax.dynamic_slice(far_down, (zero, begin), (far_down.shape[0], width))
+
     def dot(p, q):
         return jnp.dot(p, q, preferred_element_type=f32)
 
@@ -109,8 +149,11 @@
     near1_a = swap_y(own[:half], 1)
     near3_b = swap_y(own[half:], 3)
     own2 = to_twin(own)
-    acc = add_to(None, (own, 0, 0))
-    acc = add_to(acc, (own2, 0, 1))
+    acc = tuple(dot(own, lax.dynamic_slice(w, (core_rows, zero), (width, w.shape[1]))) for w in (pair_gate, pair_up))
+    acc = tuple(
+        part + dot(own2, lax.dynamic_slice(w, (twin_rows, zero), (width, w.shape[1])))
+        for part, w in zip(acc, (pair_gate, pair_up))
+    )
     far_a = swap_y(near3_a, 1)
     far_b = swap_y(near1_b, 3)
     near1 = jnp.concatenate([near1_a, near1_b], axis=0)
@@ -126,8 +169,8 @@
     hidden = (jax.nn.silu(gate_act) * up_act).astype(bf)
 
     def summed(k):
-        other = dot(hidden, cols_of(wd, k, 1)).astype(bf)
-        return dot(hidden, cols_of(wd, k, 0)) + to_twin(other).astype(f32)
+        other = dot(hidden, far_cols(twin_rows) if k == 2 else cols_of(wd, k, 1)).astype(bf)
+        return dot(hidden, far_cols(core_rows) if k == 2 else cols_of(wd, k, 0)) + to_twin(other).astype(f32)
 
     far = summed(2).astype(bf)
     got_a = swap_y(far[:half], 3)
@@ -142,12 +185,14 @@
     reduced = mine + jnp.concatenate(
         [from1_a.astype(f32) + from3_a.astype(f32), from1_b.astype(f32) + from3_b.astype(f32)], axis=0
     )
-    reduced, weights = lax.optimization_barrier((reduced.astype(bf), weights))
+    high = lax.reduce_precision(weights, 8, 7)
+    terms = jnp.concatenate([high, weights - high], axis=0).astype(bf)
+    reduced, terms = lax.optimization_barrier((reduced.astype(bf), terms))
     returned = lax.all_to_all(
         reduced.reshape(-1, capacity, width), "dp", split_axis=0, concat_axis=0, tiled=True
-    )
-    mixed = jnp.dot(weights, returned.reshape(total, width).astype(f32), precision=HIGHEST, preferred_element_type=f32)
-    return mixed.astype(bf)
+    ).reshape(total, width)
+    mixed = jnp.dot(terms, returned, preferred_element_type=f32)
+    return (mixed[:rows] + mixed[rows:]).astype(bf)
 
 
 def solution(mesh):

time: 101 us -> 104 us (1.030)
  blocking collectives: 29.7 us -> 12.7 us
  starting transfers between devices: 20.5 us -> 28.3 us
  waiting for transfers between devices: 23.1 us -> 28.8 us
  local copies, waits for them, and re-layouts: 2.41 us -> 5.08 us
  Pallas kernels: 1.87 us -> 4.51 us
    all_to_all x1 -> x0, blocking collectives: 17.1 us -> none  [on_device(): lax.all_to_all(sent.reshape(-1, capacity, width), 'dp', split_axis=0, con...]
    all_to_all x0 -> x1, starting transfers between devices: none -> 7.87 us  [on_device(): lax.all_to_all(sent.reshape(-1, capacity, width), 'dp', split_axis=0, con...]
    all_to_all x0 -> x1, waiting for transfers between devices: none -> 4 us  [on_device(): lax.all_to_all(sent.reshape(-1, capacity, width), 'dp', split_axis=0, con...]
    unnamed x13 -> x23, local copies, waits for them, and re-layouts: 2.29 us -> 4.96 us
    pallas_call x0 -> x1, Pallas kernels: none -> 2.64 us  [on_device(): pl.pallas_call(load_kernel, in_specs=[pl.BlockSpec(memory_space=pltpu.SME...]
    ppermute x15, waiting for transfers between devices: 22.5 us -> 23.8 us  [swap_y(): return lax.ppermute(v, 'tensor', [(s, s ^ 2 * k) for s in range(n_t)])]
  transfers between devices with their start and end apart: 24 -> 25, of which waited for: 10 -> 11; matrix products, arithmetic and copies ran while one was open for 17% -> 18% of each run, Pallas kernels for 0% -> 3%
where the time goes in v2:
time: 104 us
  waiting for transfers between devices  28.8 us (28%)
  starting transfers between devices  28.3 us (27%)
  matrix products  21.6 us (21%)
  blocking collectives  12.7 us (12%)
  local copies, waits for them, and re-layouts  5.08 us (5%)
  Pallas kernels  4.51 us (4%)
  other arithmetic  2.52 us (2%)
    ppermute x15, waiting for transfers between devices, swap_y(): return lax.ppermute(v, 'tensor', [(s, s ^ 2 * k) for s in range(n_t)])  23.8 us
    dot_general x24, matrix products, dot(): return jnp.dot(p, q, preferred_element_type=f32)  19.7 us
    ppermute x15, starting transfers between devices, swap_y(): return lax.ppermute(v, 'tensor', [(s, s ^ 2 * k) for s in range(n_t)])  18.3 us
    all_to_all x1, blocking collectives, on_device(): lax.all_to_all(reduced.reshape(-1, capacity, width), 'dp', split_axis=0,...  12.7 us
    all_to_all x1, starting transfers between devices, on_device(): lax.all_to_all(sent.reshape(-1, capacity, width), 'dp', split_axis=0, con...  7.87 us
    unnamed x23, local copies, waits for them, and re-layouts  4.96 us
    all_to_all x1, waiting for transfers between devices, on_device(): lax.all_to_all(sent.reshape(-1, capacity, width), 'dp', split_axis=0, con...  4 us
    pallas_call x1, Pallas kernels, on_device(): pl.pallas_call(load_kernel, in_specs=[pl.BlockSpec(memory_space=pltpu.SME...  2.64 us
  transfers between devices with their start and end apart: 25, of which 11 were waited for; matrix products, arithmetic and copies ran while one was open for 18% of the time, Pallas kernels for 3%

profile of v2, /device:TPU:0, one launch (start us, length us, event | category | flops | bytes accessed | tf_op | source)
XLA Modules:
  0.0 104.1 jit_solution(5457169520247554136)
XLA Ops:
  0.0 1.9 %sums.1 = (f32[88,128]{1,0:T(8,128)S(1)}, f32[64,512]{1,0:T(8,128)S(1)}, f32[512,128]{1,0:T(8,128)S(1)}) custom-call(bf16[64,512]{1,0:T(8,128)(2,1)} %tokens, f32[1,512]{1,0:T(1,128)} %bitcast.125, f32[1,512]{1,0:T(1,128)} %bitcast.126, f32[512,128]{1,0:T(8,128)} %eraser_in.1, f32[512,128]{1,0:T(8,128)} %eraser_out.1, f32[8,512]{1,0:T(8,128)} %bitcast.123), custom_call_target="tpu_custom_call" | custom-call | tf_op jit(solution)/shard_map/sums/pallas_call | solution.py:80
  1.9 0.7 compare_select_fusion
  3.1 3.4 %collective-permute-start.1 = (f32[88,128]{1,0:T(8,128)S(1)}, f32[88,128]{1,0:T(8,128)S(1)}, u32[]{:S(2)}, u32[]{:S(2)}) collective-permute-start(f32[88,128]{1,0:T(8,128)S(1)} %add.157), channel_id=1, source_target_pairs={{0,4},{1,5},{2,6},{3,7},{4,0},{5,1},{6,2},{7,3},{8,12},{9,13},{10,... | collective-permute-start | bytes 135176 | tf_op jit(solution)/shard_map/ppermute | solution.py:70
  7.7 1.1 %collective-permute-done.1 = f32[88,128]{1,0:T(8,128)S(1)} collective-permute-done((f32[88,128]{1,0:T(8,128)S(1)}, f32[88,128]{1,0:T(8,128)S(1)}, u32[]{:S(2)}, u32[]{:S(2)}) %collective-permute-start.1) | collective-permute-done | bytes 45088 | tf_op jit(solution)/shard_map/ppermute | solution.py:70
  8.7 1.8 %collective-permute-done.2 = f32[88,128]{1,0:T(8,128)S(1)} collective-permute-done((f32[88,128]{1,0:T(8,128)S(1)}, f32[88,128]{1,0:T(8,128)S(1)}, u32[]{:S(2)}, u32[]{:S(2)}) %collective-permute-start.2) | collective-permute-done | bytes 45088 | tf_op jit(solution)/shard_map/ppermute | solution.py:70
  10.5 1.9 %collective-permute-done.3 = f32[88,128]{1,0:T(8,128)S(1)} collective-permute-done((f32[88,128]{1,0:T(8,128)S(1)}, f32[88,128]{1,0:T(8,128)S(1)}, u32[]{:S(2)}, u32[]{:S(2)}) %collective-permute-start.3) | collective-permute-done | bytes 45088 | tf_op jit(solution)/shard_map/ppermute | solution.py:70
  13.0 1.0 convolution_convert_fusion.4
  14.0 7.9 %all-to-all-start = ((bf16[16,24,512]{2,1,0:T(8,128)(2,1)}), bf16[16,24,512]{2,1,0:T(8,128)(2,1)S(1)}, u32[]{:S(2)}, u32[]{:S(2)}) async-start(bf16[16,24,512]{2,1,0:T(8,128)(2,1)} %bitcast.8), calls=%async_computation | async-start | bytes 786432 | tf_op jit(solution)/shard_map/all_to_all | solution.py:108
  21.9 2.6 %load.1 = (bf16[1024,896]{1,0:T(8,128)(2,1)S(1)}, bf16[1024,896]{1,0:T(8,128)(2,1)S(1)}, bf16[896,1024]{1,0:T(8,128)(2,1)S(1)}) custom-call(s32[1]{0:T(128)} %bitcast.1.near_first, s32[1]{0:T(128)} %bitcast.2.far_first, bf16[1,4096,896]{2,1,0:T(8,128)(2,1)} %gate.1, bf16[1,4096,896]{2,1,0:T(8,128)(2,1)} %up.1, bf16[1,896,4096]{2,1,0:T(8,128)(2,1)} %down.1), custom_call_target="tpu_custom_call" | custom-call | tf_op jit(solution)/shard_map/load/pallas_call | solution.py:87
  24.5 1.3 %copy-done = bf16[1024,896]{1,0:T(8,128)(2,1)} copy-done((bf16[1024,896]{1,0:T(8,128)(2,1)}, bf16[1024,896]{1,0:T(8,128)(2,1)S(1)}, u32[]{:S(2)}) %copy-start) | copy-done | bytes 1835032
  25.8 1.2 %copy-done.2 = bf16[896,1024]{1,0:T(8,128)(2,1)} copy-done((bf16[896,1024]{1,0:T(8,128)(2,1)}, bf16[896,1024]{1,0:T(8,128)(2,1)S(1)}, u32[]{:S(2)}) %copy-start.2) | copy-done | bytes 1835032
  27.0 4.0 %all-to-all-done = bf16[16,24,512]{2,1,0:T(8,128)(2,1)S(1)} async-done(((bf16[16,24,512]{2,1,0:T(8,128)(2,1)}), bf16[16,24,512]{2,1,0:T(8,128)(2,1)S(1)}, u32[]{:S(2)}, u32[]{:S(2)}) %all-to-all-start) | async-done | bytes 393248 | tf_op jit(solution)/shard_map/all_to_all | solution.py:108
  31.0 0.7 collective-permute-start.9
  31.8 2.6 %collective-permute-start.4 = (bf16[192,512]{1,0:T(8,128)(2,1)S(1)}, bf16[192,512]{1,0:T(8,128)(2,1)S(1)}, u32[]{:S(2)}, u32[]{:S(2)}) collective-permute-start(bf16[192,512]{1,0:T(8,128)(2,1)S(1)} %get-tuple-element.74), channel_id=1, source_target_pairs={{0,6},{1,7},{2,4},{3,5},{4,2},{5,3},{6,0},{7,1},{8,14},{9,15},{10,... | collective-permute-start | bytes 589832 | tf_op jit(solution)/shard_map/ppermute | solution.py:70
  34.4 1.4 %collective-permute-start.8 = (bf16[192,512]{1,0:T(8,128)(2,1)S(1)}, bf16[192,512]{1,0:T(8,128)(2,1)S(1)}, u32[]{:S(2)}, u32[]{:S(2)}) collective-permute-start(bf16[192,512]{1,0:T(8,128)(2,1)S(1)} %get-tuple-element.74), channel_id=1, source_target_pairs={{0,2},{1,3},{2,0},{3,1},{4,6},{5,7},{6,4},{7,5},{8,10},{9,11},{10,... | collective-permute-start | bytes 589832 | tf_op jit(solution)/shard_map/ppermute | solution.py:70
  35.8 1.8 %fusion.75 = f32[384,896]{1,0:T(8,128)S(1)} fusion(bf16[384,512]{1,0:T(8,128)(2,1)S(1)} %bitcast.119, bf16[1024,896]{1,0:T(8,128)(2,1)} %copy-done, u32[]{:T(128)S(6)} %mul.110), kind=kOutput, calls=%fused_computation.75 | convolution fusion | flops 352321536 | bytes 2686980 | tf_op jit(solution)/shard_map/dot_general | solution.py:138
  38.7 5.2 %collective-permute-done.4 = bf16[192,512]{1,0:T(8,128)(2,1)S(1)} collective-permute-done((bf16[192,512]{1,0:T(8,128)(2,1)S(1)}, bf16[192,512]{1,0:T(8,128)(2,1)S(1)}, u32[]{:S(2)}, u32[]{:S(2)}) %collective-permute-start.4) | collective-permute-done | bytes 196640 | tf_op jit(solution)/shard_map/ppermute | solution.py:70
  46.0 2.4 %fusion.39 = f32[384,896]{1,0:T(8,128)S(1)} fusion(bf16[384,512]{1,0:T(8,128)(2,1)S(1)} %pad_maximum_fusion, bf16[1,4096,896]{2,1,0:T(8,128)(2,1)} %up.1, u32[]{:T(128)S(6)} %mul.115), kind=kOutput, calls=%fused_computation.43 | convolution fusion | flops 352321536 | bytes 2686980 | tf_op jit(solution)/shard_map/dot_general | solution.py:138
  48.4 0.7 collective-permute-start.12
  49.1 2.0 %convolution_add_fusion.1 = f32[384,896]{1,0:T(8,128)S(1)} fusion(bf16[384,512]{1,0:T(8,128)(2,1)S(1)} %pad_maximum_fusion.1, f32[384,896]{1,0:T(8,128)S(1)} %convolution_add_fusion.4, f32[384,896]{1,0:T(8,128)S(1)} %fusion.39, bf16[1,4096,896]{2,1,0:T(8,128)(2,1)} %up.1, u32[]{:T(128)S(6)} %mul.119), kind=kOutput, calls=%fused_computation.1 | convolution fusion | flops 353009664 | bytes 5439492 | tf_op jit(solution)/shard_map/dot_general | solution.py:138
  58.9 1.7 %slice-done.5 = s8[4194304]{0:T(1024)(128)(4,1)S(1)} async-done(((s8[7340032]{0:T(1024)(128)(4,1)}), s8[4194304]{0:T(1024)(128)(4,1)S(1)}, s32[]{:S(2)}) %slice-start.5) | async-done | bytes 4194328
  63.0 0.7 convolution_convert_fusion
  64.2 0.7 convolution_convert_fusion.3
  65.8 2.7 %collective-permute-start.17 = (bf16[192,512]{1,0:T(8,128)(2,1)S(1)}, bf16[192,512]{1,0:T(8,128)(2,1)S(1)}, u32[]{:S(2)}, u32[]{:S(2)}) collective-permute-start(bf16[192,512]{1,0:T(8,128)(2,1)S(1)} %get-tuple-element.71), channel_id=1, source_target_pairs={{0,6},{1,7},{2,4},{3,5},{4,2},{5,3},{6,0},{7,1},{8,14},{9,15},{10,... | collective-permute-start | bytes 589832 | tf_op jit(solution)/shard_map/ppermute | solution.py:70
  69.2 0.7 collective-permute-start.20
  71.0 1.8 %collective-permute-start.22 = (bf16[192,512]{1,0:T(8,128)(2,1)S(1)}, bf16[192,512]{1,0:T(8,128)(2,1)S(1)}, u32[]{:S(2)}, u32[]{:S(2)}) collective-permute-start(bf16[192,512]{1,0:T(8,128)(2,1)S(1)} %get-tuple-element.72), channel_id=1, source_target_pairs={{0,2},{1,3},{2,0},{3,1},{4,6},{5,7},{6,4},{7,5},{8,10},{9,11},{10,... | collective-permute-start | bytes 589832 | tf_op jit(solution)/shard_map/ppermute | solution.py:70
  72.8 2.1 %collective-permute-done.17 = bf16[192,512]{1,0:T(8,128)(2,1)S(1)} collective-permute-done((bf16[192,512]{1,0:T(8,128)(2,1)S(1)}, bf16[192,512]{1,0:T(8,128)(2,1)S(1)}, u32[]{:S(2)}, u32[]{:S(2)}) %collective-permute-start.17) | collective-permute-done | bytes 196640 | tf_op jit(solution)/shard_map/ppermute | solution.py:70
  75.2 7.5 %collective-permute-done.22 = bf16[192,512]{1,0:T(8,128)(2,1)S(1)} collective-permute-done((bf16[192,512]{1,0:T(8,128)(2,1)S(1)}, bf16[192,512]{1,0:T(8,128)(2,1)S(1)}, u32[]{:S(2)}, u32[]{:S(2)}) %collective-permute-start.22) | collective-permute-done | bytes 196640 | tf_op jit(solution)/shard_map/ppermute | solution.py:70
  82.8 2.7 %collective-permute-start.23 = (bf16[192,512]{1,0:T(8,128)(2,1)S(1)}, bf16[192,512]{1,0:T(8,128)(2,1)S(1)}, u32[]{:S(2)}, u32[]{:S(2)}) collective-permute-start(bf16[192,512]{1,0:T(8,128)(2,1)S(1)} %fusion.80), channel_id=1, source_target_pairs={{0,6},{1,7},{2,4},{3,5},{4,2},{5,3},{6,0},{7,1},{8,14},{9,15},{10,... | collective-permute-start | bytes 589832 | tf_op jit(solution)/shard_map/ppermute | solution.py:70
  85.9 3.9 %collective-permute-done.23 = bf16[192,512]{1,0:T(8,128)(2,1)S(1)} collective-permute-done((bf16[192,512]{1,0:T(8,128)(2,1)S(1)}, bf16[192,512]{1,0:T(8,128)(2,1)S(1)}, u32[]{:S(2)}, u32[]{:S(2)}) %collective-permute-start.23) | collective-permute-done | bytes 196640 | tf_op jit(solution)/shard_map/ppermute | solution.py:70
  89.8 0.7 fusion.24
  90.5 12.7 %all_to_all.10 = bf16[16,24,512]{2,1,0:T(8,128)(2,1)S(1)} all-to-all(bf16[16,24,512]{2,1,0:T(8,128)(2,1)S(1)} %bitcast.122), channel_id=1, replica_groups=mesh['dp'=16,'tensor'=8] {'dp'}, dimensions={0} | all-to-all | bytes 786432 | tf_op jit(solution)/shard_map/all_to_all | solution.py:191
  (103 shorter events, 20.2 us)
Async XLA Ops:
  1.9 1.2 %collective-permute-start = (f32[88,128]{1,0:T(8,128)S(1)}, f32[88,128]{1,0:T(8,128)S(1)}, u32[]{:S(2)}, u32[]{:S(2)}) collective-permute-start(f32[88,128]{1,0:T(8,128)S(1)} %get-tuple-element.38), channel_id=1, source_target_pairs={{0,1},{1,0},{2,3},{3,2},{4,5},{5,4},{6,7},{7,6},{8,9},{9,8},{10,11... | collective-permute-start | bytes 135176 | tf_op jit(solution)/shard_map/ppermute | solution.py:73
  3.1 5.6 %collective-permute-start.1 = (f32[88,128]{1,0:T(8,128)S(1)}, f32[88,128]{1,0:T(8,128)S(1)}, u32[]{:S(2)}, u32[]{:S(2)}) collective-permute-start(f32[88,128]{1,0:T(8,128)S(1)} %add.157), channel_id=1, source_target_pairs={{0,4},{1,5},{2,6},{3,7},{4,0},{5,1},{6,2},{7,3},{8,12},{9,13},{10,... | collective-permute-start | bytes 135176 | tf_op jit(solution)/shard_map/ppermute | solution.py:70
  6.5 4.0 %collective-permute-start.2 = (f32[88,128]{1,0:T(8,128)S(1)}, f32[88,128]{1,0:T(8,128)S(1)}, u32[]{:S(2)}, u32[]{:S(2)}) collective-permute-start(f32[88,128]{1,0:T(8,128)S(1)} %add.157), channel_id=1, source_target_pairs={{0,2},{1,3},{2,0},{3,1},{4,6},{5,7},{6,4},{7,5},{8,10},{9,11},{10,... | collective-permute-start | bytes 135176 | tf_op jit(solution)/shard_map/ppermute | solution.py:70
  7.2 5.3 %collective-permute-start.3 = (f32[88,128]{1,0:T(8,128)S(1)}, f32[88,128]{1,0:T(8,128)S(1)}, u32[]{:S(2)}, u32[]{:S(2)}) collective-permute-start(f32[88,128]{1,0:T(8,128)S(1)} %add.157), channel_id=1, source_target_pairs={{0,6},{1,7},{2,4},{3,5},{4,2},{5,3},{6,0},{7,1},{8,14},{9,15},{10,... | collective-permute-start | bytes 135176 | tf_op jit(solution)/shard_map/ppermute | solution.py:70
  14.0 17.0 %all-to-all-start = ((bf16[16,24,512]{2,1,0:T(8,128)(2,1)}), bf16[16,24,512]{2,1,0:T(8,128)(2,1)S(1)}, u32[]{:S(2)}, u32[]{:S(2)}) async-start(bf16[16,24,512]{2,1,0:T(8,128)(2,1)} %bitcast.8), calls=%async_computation | async-start | bytes 786432 | tf_op jit(solution)/shard_map/all_to_all | solution.py:108
  31.0 13.6 %collective-permute-start.10 = (bf16[384,512]{1,0:T(8,128)(2,1)S(1)}, bf16[384,512]{1,0:T(8,128)(2,1)S(1)}, u32[]{:S(2)}, u32[]{:S(2)}) collective-permute-start(bf16[384,512]{1,0:T(8,128)(2,1)S(1)} %bitcast.117), channel_id=1, source_target_pairs={{0,1},{1,0},{2,3},{3,2},{4,5},{5,4},{6,7},{7,6},{8,9},{9,8},{10,11... | collective-permute-start | bytes 1179656 | tf_op jit(solution)/shard_map/ppermute | solution.py:73
  31.0 13.5 %collective-permute-start.9 = (bf16[192,512]{1,0:T(8,128)(2,1)S(1)}, bf16[192,512]{1,0:T(8,128)(2,1)S(1)}, u32[]{:S(2)}, u32[]{:S(2)}) collective-permute-start(bf16[192,512]{1,0:T(8,128)(2,1)S(1)} %get-tuple-element.73), channel_id=1, source_target_pairs={{0,6},{1,7},{2,4},{3,5},{4,2},{5,3},{6,0},{7,1},{8,14},{9,15},{10,... | collective-permute-start | bytes 589832 | tf_op jit(solution)/shard_map/ppermute | solution.py:70
  31.8 12.1 %collective-permute-start.6 = (bf16[192,512]{1,0:T(8,128)(2,1)S(1)}, bf16[192,512]{1,0:T(8,128)(2,1)S(1)}, u32[]{:S(2)}, u32[]{:S(2)}) collective-permute-start(bf16[192,512]{1,0:T(8,128)(2,1)S(1)} %get-tuple-element.73), channel_id=1, source_target_pairs={{0,2},{1,3},{2,0},{3,1},{4,6},{5,7},{6,4},{7,5},{8,10},{9,11},{10,... | collective-permute-start | bytes 589832 | tf_op jit(solution)/shard_map/ppermute | solution.py:70
  31.8 12.1 %collective-permute-start.4 = (bf16[192,512]{1,0:T(8,128)(2,1)S(1)}, bf16[192,512]{1,0:T(8,128)(2,1)S(1)}, u32[]{:S(2)}, u32[]{:S(2)}) collective-permute-start(bf16[192,512]{1,0:T(8,128)(2,1)S(1)} %get-tuple-element.74), channel_id=1, source_target_pairs={{0,6},{1,7},{2,4},{3,5},{4,2},{5,3},{6,0},{7,1},{8,14},{9,15},{10,... | collective-permute-start | bytes 589832 | tf_op jit(solution)/shard_map/ppermute | solution.py:70
  34.4 10.2 %collective-permute-start.8 = (bf16[192,512]{1,0:T(8,128)(2,1)S(1)}, bf16[192,512]{1,0:T(8,128)(2,1)S(1)}, u32[]{:S(2)}, u32[]{:S(2)}) collective-permute-start(bf16[192,512]{1,0:T(8,128)(2,1)S(1)} %get-tuple-element.74), channel_id=1, source_target_pairs={{0,2},{1,3},{2,0},{3,1},{4,6},{5,7},{6,4},{7,5},{8,10},{9,11},{10,... | collective-permute-start | bytes 589832 | tf_op jit(solution)/shard_map/ppermute | solution.py:70
  38.2 6.4 %copy-start.1 = (bf16[1024,896]{1,0:T(8,128)(2,1)S(1)}, bf16[1024,896]{1,0:T(8,128)(2,1)}, u32[]{:S(2)}) copy-start(bf16[1024,896]{1,0:T(8,128)(2,1)} %copy-done) | copy-start | bytes 5505028
  43.9 11.1 %collective-permute-start.5 = (bf16[192,512]{1,0:T(8,128)(2,1)S(1)}, bf16[192,512]{1,0:T(8,128)(2,1)S(1)}, u32[]{:S(2)}, u32[]{:S(2)}) collective-permute-start(bf16[192,512]{1,0:T(8,128)(2,1)S(1)} %collective-permute-done.4), channel_id=1, source_target_pairs={{0,2},{1,3},{2,0},{3,1},{4,6},{5,7},{6,4},{7,5},{8,10},{9,11},{10,... | collective-permute-start | bytes 589832 | tf_op jit(solution)/shard_map/ppermute | solution.py:70
  43.9 11.1 %collective-permute-start.7 = (bf16[192,512]{1,0:T(8,128)(2,1)S(1)}, bf16[192,512]{1,0:T(8,128)(2,1)S(1)}, u32[]{:S(2)}, u32[]{:S(2)}) collective-permute-start(bf16[192,512]{1,0:T(8,128)(2,1)S(1)} %collective-permute-done.6), channel_id=1, source_target_pairs={{0,6},{1,7},{2,4},{3,5},{4,2},{5,3},{6,0},{7,1},{8,14},{9,15},{10,... | collective-permute-start | bytes 589832 | tf_op jit(solution)/shard_map/ppermute | solution.py:70
  44.6 6.5 %slice-start = ((s8[7340032]{0:T(1024)(128)(4,1)}), s8[3145728]{0:T(1024)(128)(4,1)S(1)}, s32[]{:S(2)}) async-start(s8[7340032]{0:T(1024)(128)(4,1)} %bitcast.111), calls=%async_computation.2 | async-start | bytes 6291456
  45.3 7.2 %slice-start.2 = ((s8[7340032]{0:T(1024)(128)(4,1)}), s8[4194304]{0:T(1024)(128)(4,1)S(1)}, s32[]{:S(2)}) async-start(s8[7340032]{0:T(1024)(128)(4,1)} %bitcast.113), calls=%async_computation.4 | async-start | bytes 8388608
  45.9 5.2 %slice-start.1 = ((s8[7340032]{0:T(1024)(128)(4,1)}), s8[4194304]{0:T(1024)(128)(4,1)S(1)}, s32[]{:S(2)}) async-start(s8[7340032]{0:T(1024)(128)(4,1)} %bitcast.111), calls=%async_computation.3 | async-start | bytes 8388608
  45.9 7.8 %collective-permute-start.11 = (bf16[384,512]{1,0:T(8,128)(2,1)S(1)}, bf16[384,512]{1,0:T(8,128)(2,1)S(1)}, u32[]{:S(2)}, u32[]{:S(2)}) collective-permute-start(bf16[384,512]{1,0:T(8,128)(2,1)S(1)} %pad_maximum_fusion), channel_id=1, source_target_pairs={{0,1},{1,0},{2,3},{3,2},{4,5},{5,4},{6,7},{7,6},{8,9},{9,8},{10,11... | collective-permute-start | bytes 1179656 | tf_op jit(solution)/shard_map/ppermute | solution.py:73
  48.4 4.0 %slice-start.3 = ((s8[7340032]{0:T(1024)(128)(4,1)}), s8[3145728]{0:T(1024)(128)(4,1)S(1)}, s32[]{:S(2)}) async-start(s8[7340032]{0:T(1024)(128)(4,1)} %bitcast.113), calls=%async_computation.5 | async-start | bytes 6291456
  48.4 4.0 %collective-permute-start.12 = (bf16[384,512]{1,0:T(8,128)(2,1)S(1)}, bf16[384,512]{1,0:T(8,128)(2,1)S(1)}, u32[]{:S(2)}, u32[]{:S(2)}) collective-permute-start(bf16[384,512]{1,0:T(8,128)(2,1)S(1)} %pad_maximum_fusion.1), channel_id=1, source_target_pairs={{0,1},{1,0},{2,3},{3,2},{4,5},{5,4},{6,7},{7,6},{8,9},{9,8},{10,11... | collective-permute-start | bytes 1179656 | tf_op jit(solution)/shard_map/ppermute | solution.py:73
  55.0 2.0 %collective-permute-start.13 = (bf16[384,512]{1,0:T(8,128)(2,1)S(1)}, bf16[384,512]{1,0:T(8,128)(2,1)S(1)}, u32[]{:S(2)}, u32[]{:S(2)}) collective-permute-start(bf16[384,512]{1,0:T(8,128)(2,1)S(1)} %constant_dynamic-update-slice_fusion), channel_id=1, source_target_pairs={{0,1},{1,0},{2,3},{3,2},{4,5},{5,4},{6,7},{7,6},{8,9},{9,8},{10,11... | collective-permute-start | bytes 1179656 | tf_op jit(solution)/shard_map/ppermute | solution.py:73
  57.0 1.9 %slice-start.4 = ((s8[7340032]{0:T(1024)(128)(4,1)}), s8[3145728]{0:T(1024)(128)(4,1)S(1)}, s32[]{:S(2)}) async-start(s8[7340032]{0:T(1024)(128)(4,1)} %bitcast.115), calls=%async_computation.6 | async-start | bytes 6291456
  58.2 2.4 %slice-start.5 = ((s8[7340032]{0:T(1024)(128)(4,1)}), s8[4194304]{0:T(1024)(128)(4,1)S(1)}, s32[]{:S(2)}) async-start(s8[7340032]{0:T(1024)(128)(4,1)} %bitcast.115), calls=%async_computation.7 | async-start | bytes 8388608
  61.3 8.7 %collective-permute-start.15 = (bf16[384,512]{1,0:T(8,128)(2,1)S(1)}, bf16[384,512]{1,0:T(8,128)(2,1)S(1)}, u32[]{:S(2)}, u32[]{:S(2)}) collective-permute-start(bf16[384,512]{1,0:T(8,128)(2,1)S(1)} %convolution_convert_fusion.2), channel_id=1, source_target_pairs={{0,1},{1,0},{2,3},{3,2},{4,5},{5,4},{6,7},{7,6},{8,9},{9,8},{10,11... | collective-permute-start | bytes 1179656 | tf_op jit(solution)/shard_map/ppermute | solution.py:73
  62.8 2.3 %collective-permute-start.16 = (bf16[384,512]{1,0:T(8,128)(2,1)S(1)}, bf16[384,512]{1,0:T(8,128)(2,1)S(1)}, u32[]{:S(2)}, u32[]{:S(2)}) collective-permute-start(bf16[384,512]{1,0:T(8,128)(2,1)S(1)} %convolution_convert_fusion.1), channel_id=1, source_target_pairs={{0,1},{1,0},{2,3},{3,2},{4,5},{5,4},{6,7},{7,6},{8,9},{9,8},{10,11... | collective-permute-start | bytes 1179656 | tf_op jit(solution)/shard_map/ppermute | solution.py:73
  63.7 4.8 %collective-permute-start.19 = (bf16[384,512]{1,0:T(8,128)(2,1)S(1)}, bf16[384,512]{1,0:T(8,128)(2,1)S(1)}, u32[]{:S(2)}, u32[]{:S(2)}) collective-permute-start(bf16[384,512]{1,0:T(8,128)(2,1)S(1)} %convolution_convert_fusion), channel_id=1, source_target_pairs={{0,1},{1,0},{2,3},{3,2},{4,5},{5,4},{6,7},{7,6},{8,9},{9,8},{10,11... | collective-permute-start | bytes 1179656 | tf_op jit(solution)/shard_map/ppermute | solution.py:73
  64.9 25.0 %collective-permute-start.14 = (bf16[384,512]{1,0:T(8,128)(2,1)S(1)}, bf16[384,512]{1,0:T(8,128)(2,1)S(1)}, u32[]{:S(2)}, u32[]{:S(2)}) collective-permute-start(bf16[384,512]{1,0:T(8,128)(2,1)S(1)} %convolution_convert_fusion.3), channel_id=1, source_target_pairs={{0,1},{1,0},{2,3},{3,2},{4,5},{5,4},{6,7},{7,6},{8,9},{9,8},{10,11... | collective-permute-start | bytes 1179656 | tf_op jit(solution)/shard_map/ppermute | solution.py:73
  65.8 9.1 %collective-permute-start.17 = (bf16[192,512]{1,0:T(8,128)(2,1)S(1)}, bf16[192,512]{1,0:T(8,128)(2,1)S(1)}, u32[]{:S(2)}, u32[]{:S(2)}) collective-permute-start(bf16[192,512]{1,0:T(8,128)(2,1)S(1)} %get-tuple-element.71), channel_id=1, source_target_pairs={{0,6},{1,7},{2,4},{3,5},{4,2},{5,3},{6,0},{7,1},{8,14},{9,15},{10,... | collective-permute-start | bytes 589832 | tf_op jit(solution)/shard_map/ppermute | solution.py:70
  69.2 16.3 %collective-permute-start.20 = (bf16[192,512]{1,0:T(8,128)(2,1)S(1)}, bf16[192,512]{1,0:T(8,128)(2,1)S(1)}, u32[]{:S(2)}, u32[]{:S(2)}) collective-permute-start(bf16[192,512]{1,0:T(8,128)(2,1)S(1)} %slice.126), channel_id=1, source_target_pairs={{0,6},{1,7},{2,4},{3,5},{4,2},{5,3},{6,0},{7,1},{8,14},{9,15},{10,... | collective-permute-start | bytes 589832 | tf_op jit(solution)/shard_map/ppermute | solution.py:70
  70.7 15.2 %collective-permute-start.21 = (bf16[192,512]{1,0:T(8,128)(2,1)S(1)}, bf16[192,512]{1,0:T(8,128)(2,1)S(1)}, u32[]{:S(2)}, u32[]{:S(2)}) collective-permute-start(bf16[192,512]{1,0:T(8,128)(2,1)S(1)} %slice.125), channel_id=1, source_target_pairs={{0,2},{1,3},{2,0},{3,1},{4,6},{5,7},{6,4},{7,5},{8,10},{9,11},{10,... | collective-permute-start | bytes 589832 | tf_op jit(solution)/shard_map/ppermute | solution.py:70
  71.0 11.8 %collective-permute-start.22 = (bf16[192,512]{1,0:T(8,128)(2,1)S(1)}, bf16[192,512]{1,0:T(8,128)(2,1)S(1)}, u32[]{:S(2)}, u32[]{:S(2)}) collective-permute-start(bf16[192,512]{1,0:T(8,128)(2,1)S(1)} %get-tuple-element.72), channel_id=1, source_target_pairs={{0,2},{1,3},{2,0},{3,1},{4,6},{5,7},{6,4},{7,5},{8,10},{9,11},{10,... | collective-permute-start | bytes 589832 | tf_op jit(solution)/shard_map/ppermute | solution.py:70
  74.9 10.9 %collective-permute-start.18 = (bf16[192,512]{1,0:T(8,128)(2,1)S(1)}, bf16[192,512]{1,0:T(8,128)(2,1)S(1)}, u32[]{:S(2)}, u32[]{:S(2)}) collective-permute-start(bf16[192,512]{1,0:T(8,128)(2,1)S(1)} %fusion.81), channel_id=1, source_target_pairs={{0,2},{1,3},{2,0},{3,1},{4,6},{5,7},{6,4},{7,5},{8,10},{9,11},{10,... | collective-permute-start | bytes 589832 | tf_op jit(solution)/shard_map/ppermute | solution.py:70
  82.8 7.0 %collective-permute-start.23 = (bf16[192,512]{1,0:T(8,128)(2,1)S(1)}, bf16[192,512]{1,0:T(8,128)(2,1)S(1)}, u32[]{:S(2)}, u32[]{:S(2)}) collective-permute-start(bf16[192,512]{1,0:T(8,128)(2,1)S(1)} %fusion.80), channel_id=1, source_target_pairs={{0,6},{1,7},{2,4},{3,5},{4,2},{5,3},{6,0},{7,1},{8,14},{9,15},{10,... | collective-permute-start | bytes 589832 | tf_op jit(solution)/shard_map/ppermute | solution.py:70
  (4 other events, 4.8 us)
